TPU v7x, 32 devices: a whole 2x2x4 slice. The times are simulated.
32 devices in a mesh: gz: 16 (over z, y, core), ba: 2 (over x).
Axes of the slice: x: 2, y: 2, z: 4, core: 2. Of those that a mesh axis runs over, the one named last changes fastest.
Arguments:
- coeffs: float32 [2, 3, 4, 32, 128, 128], P(None, None, 'ba', 'gz'), may hold values from -6 to 6
- material: int32 [32, 128, 128], P('gz'), may hold values from 0 to 3
- inv_diag: float32 [4, 3], replicated, may hold values from 0.1 to 1
- inv_off: float32 [4, 3], replicated, may hold values from -0.1 to 0.1
Outputs:
- theta: float32 [2, 3, 4, 32, 128, 128], P(None, None, 'ba', 'gz')
- gram: float32 [2, 4, 4], P(None, None, 'ba')
Inputs may be any that keep to these rules, and one draw needn't show every extreme that they name: material indices.
All inputs are finite; a program needn't handle non-finite values.
Results may differ from a plain program's by a relative error of at most 0.00011.
Values sent between devices are 32-bit elements; how exact they have to be, the bound alone decides.
A program may use at most 64 MiB of HBM per device.

v0:
```python
import functools
import math

import jax
import jax.numpy as jnp
import numpy as np
from jax import lax
from jax.experimental import pallas as pl
from jax.experimental.pallas import tpu as pltpu
from jax.sharding import PartitionSpec as P

highest = lax.Precision.HIGHEST
half_turn = 3.141592653589793


def reverse_bits(values, levels):
    flipped = jnp.zeros_like(values)
    for position in range(levels):
        flipped = flipped + (values >> position & 1) * (1 << levels - 1 - position)
    return flipped


def signed_wave(numbers, length):
    shifted = jnp.where(numbers < length // 2, numbers, numbers - length)
    return shifted.astype(jnp.float32) / (length / 2.0)


def phase_tables(first, second, length, sign):
    product = first[:, None] * second[None, :] % length
    angle = 2.0 * half_turn / length * product.astype(jnp.float32)
    factor = 1.0 / math.sqrt(length)
    return (jnp.cos(angle) * factor, sign * jnp.sin(angle) * factor)


def cross_waves(waves, field):
    first, second, third = waves
    return jnp.stack(
        [
            second * field[:, 2] - third * field[:, 1],
            third * field[:, 0] - first * field[:, 2],
            first * field[:, 1] - second * field[:, 0],
        ],
        axis=1,
    )


def along_width(field, cosine, sine):
    breadth = field.shape[-1]
    rows = field.reshape(2, -1, breadth)
    joined = jnp.concatenate([cosine, sine], axis=1)
    real_prod = jnp.dot(rows[0], joined, precision=highest)
    imag_prod = jnp.dot(rows[1], joined, precision=highest)
    real_out = real_prod[:, :breadth] - imag_prod[:, breadth:]
    imag_out = real_prod[:, breadth:] + imag_prod[:, :breadth]
    return jnp.stack([real_out, imag_out]).reshape(field.shape)


def along_height(field, cosine, sine):
    tables = jnp.stack([cosine, sine])
    product = jnp.einsum("pcbzyx,tyk->tpcbzkx", field, tables, precision=highest)
    return jnp.stack([product[0, 0] - product[1, 1], product[1, 0] + product[0, 1]])


def along_depth(field, cosine, sine):
    tables = jnp.stack([cosine, sine])
    product = jnp.einsum("pcbzyx,tzk->tpcbkyx", field, tables, precision=highest)
    return jnp.stack([product[0, 0] - product[1, 1], product[1, 0] + product[0, 1]])


def apply_material(field, material, inv_diag, inv_off):
    materials = inv_diag.shape[0]
    onehot = (material[None] == jnp.arange(materials, dtype=jnp.int32)[:, None, None, None]).astype(
        jnp.float32
    )
    table = jnp.concatenate([inv_diag, inv_off], axis=1)
    tensor = jnp.einsum("mk,mzyx->kzyx", table, onehot, precision=highest)
    first = field[:, 0]
    second = field[:, 1]
    third = field[:, 2]
    return jnp.stack(
        [
            tensor[0] * first + tensor[3] * second + tensor[5] * third,
            tensor[3] * first + tensor[1] * second + tensor[4] * third,
            tensor[5] * first + tensor[4] * second + tensor[2] * third,
        ],
        axis=1,
    )


def on_device(coeffs, material, inv_diag, inv_off):
    groups = lax.axis_size("gz")
    levels = groups.bit_length() - 1
    depth = coeffs.shape[3]
    height = coeffs.shape[4]
    breadth = coeffs.shape[5]
    total_depth = depth * groups
    device = lax.axis_index("gz")
    local_rows = jnp.arange(depth, dtype=jnp.int32)
    waves_here = reverse_bits(device, levels) + groups * local_rows
    across = jnp.arange(breadth, dtype=jnp.int32)
    upward = jnp.arange(height, dtype=jnp.int32)
    waves = (
        signed_wave(across, breadth)[None, None, :],
        signed_wave(upward, height)[None, :, None],
        signed_wave(waves_here, total_depth)[:, None, None],
    )
    curl = cross_waves(waves, coeffs)
    all_rows = jnp.arange(total_depth, dtype=jnp.int32)
    wave_rows = reverse_bits(all_rows // depth, levels) + groups * (all_rows % depth)
    height_cos, height_sin = phase_tables(upward, upward, height, 1.0)
    width_cos, width_sin = phase_tables(across, across, breadth, 1.0)
    planar = along_height(curl, height_cos, height_sin)
    planar = along_width(planar, width_cos, width_sin)
    material_slab = lax.all_to_all(material, "gz", split_axis=1, concat_axis=0, tiled=True)
    inverse_cos, inverse_sin = phase_tables(wave_rows, all_rows, total_depth, 1.0)
    forward_cos, forward_sin = phase_tables(all_rows, wave_rows, total_depth, -1.0)
    spatial_piece = along_depth(
        lax.all_to_all(planar, "gz", split_axis=4, concat_axis=3, tiled=True),
        inverse_cos,
        inverse_sin,
    )
    scaled_piece = apply_material(spatial_piece, material_slab, inv_diag, inv_off)
    returned = along_depth(scaled_piece, forward_cos, forward_sin)
    spectral = lax.all_to_all(returned, "gz", split_axis=3, concat_axis=4, tiled=True)
    spectral = along_width(spectral, width_cos, -width_sin)
    spectral = along_height(spectral, height_cos, -height_sin)
    theta = -cross_waves(waves, spectral)
    factor = 1.0 / (breadth * height * total_depth)
    piece = lax.all_gather(coeffs, "ba", axis=2, tiled=True)
    real_part = jnp.einsum("cbzyx,cezyx->be", piece[0], theta[0], precision=highest) + jnp.einsum(
        "cbzyx,cezyx->be", piece[1], theta[1], precision=highest
    )
    imag_part = jnp.einsum("cbzyx,cezyx->be", piece[0], theta[1], precision=highest) - jnp.einsum(
        "cbzyx,cezyx->be", piece[1], theta[0], precision=highest
    )
    block = jnp.stack([real_part, imag_part]) * factor
    gram = lax.psum(block, "gz")
    return (theta, gram)


MESH = pl.DeviceIdType.MESH
single = jnp.float32
half = jnp.bfloat16


def split_table(length, extra):
    numbers = np.arange(length)
    angle = 2.0 * np.pi / length * (numbers[:, None] * numbers[None, :] % length)
    cosine = np.cos(angle) * extra / math.sqrt(length)
    sine = np.sin(angle) * extra / math.sqrt(length)
    inverse = np.block([[cosine, sine], [-sine, cosine]])
    parts = []
    for table in (inverse, inverse.T):
        high = table.astype(np.float32).astype(half)
        low = (table - high.astype(np.float64)).astype(half)
        parts += [high, low]
    return np.stack(parts)


def halves(values):
    high = values.astype(half)
    return high, (values - high.astype(single)).astype(half)


def product(first, second):
    dot = functools.partial(jnp.dot, preferred_element_type=single)
    return dot(first[0], second[0]) + (dot(first[0], second[1]) + dot(first[1], second[0]))


def twiddled(pair, step, span, sign):
    real, imag = pair
    if step == 0:
        return real, imag
    if 2 * step == span:
        return (-imag, real) if sign > 0 else (imag, -real)
    angle = math.pi * step / span
    cosine, sine = math.cos(angle), sign * math.sin(angle)
    return real * cosine - imag * sine, real * sine + imag * cosine


def to_voxels(points):
    points = list(points)
    span = 1
    while span < len(points):
        for base in range(0, len(points), 2 * span):
            for step in range(span):
                a = points[base + step]
                t = twiddled(points[base + step + span], step, span, 1.0)
                points[base + step] = (a[0] + t[0], a[1] + t[1])
                points[base + step + span] = (a[0] - t[0], a[1] - t[1])
        span *= 2
    return points


def to_waves(points):
    points = list(points)
    span = len(points) // 2
    while span >= 1:
        for base in range(0, len(points), 2 * span):
            for step in range(span):
                a, t = points[base + step], points[base + step + span]
                points[base + step] = (a[0] + t[0], a[1] + t[1])
                points[base + step + span] = twiddled(
                    (a[0] - t[0], a[1] - t[1]), step, span, -1.0
                )
        span //= 2
    return points


def operator_kernel(
    groups,
    coeffs_hbm,
    material_hbm,
    diag_hbm,
    off_hbm,
    table_hbm,
    theta_ref,
    gram_ref,
    coeffs_ref,
    material_ref,
    table_ref,
    diag_ref,
    off_ref,
    slab_ref,
    tensor_ref,
    high_ref,
    low_ref,
    back_ref,
    field_ref,
    scaled_ref,
    other_ref,
    out1_ref,
    in1_ref,
    out2_ref,
    in2_ref,
    sums_ref,
    load_sem,
    slab_send,
    slab_recv,
    half_sem,
    send1,
    recv1,
    send2,
    recv2,
    other_send,
    other_recv,
    sums_send,
    sums_recv,
):
    _, comps, bands, depth, height, breadth = coeffs_ref.shape
    total = depth * groups
    columns = height // groups
    levels = groups.bit_length() - 1
    me = lax.axis_index("gz")
    mine = lax.axis_index("ba")
    middle = groups // 2

    def offset_of(i):
        away = (i + 1) // 2
        return middle + away - 2 * away * (i % 2)

    def each_peer(body):
        def step(i, carry):
            k = offset_of(i)
            body(k, (me + k) % groups, (me + groups - k) % groups)
            return carry

        lax.fori_loop(0, groups - 1, step, 0)

    barrier = pltpu.get_barrier_semaphore()
    each_peer(
        lambda k, peer, source: pl.semaphore_signal(
            barrier, inc=1, device_id={"gz": peer}, device_id_type=MESH
        )
    )
    pl.semaphore_signal(barrier, inc=1, device_id={"ba": 1 - mine}, device_id_type=MESH)

    loads = [
        pltpu.make_async_copy(coeffs_hbm, coeffs_ref, load_sem.at[0]),
        pltpu.make_async_copy(table_hbm, table_ref, load_sem.at[1]),
        pltpu.make_async_copy(material_hbm, material_ref, load_sem.at[2]),
        pltpu.make_async_copy(diag_hbm, diag_ref, load_sem.at[3]),
        pltpu.make_async_copy(off_hbm, off_ref, load_sem.at[4]),
    ]
    for load in loads:
        load.start()

    across = lax.broadcasted_iota(jnp.int32, (1, breadth), 1)
    upward = lax.broadcasted_iota(jnp.int32, (height, 1), 0)
    wave_x = jnp.where(across < breadth // 2, across, across - breadth).astype(single) / (
        breadth / 2.0
    )
    wave_y = jnp.where(upward < height // 2, upward, upward - height).astype(single) / (
        height / 2.0
    )
    reversed_me = 0
    for position in range(levels):
        reversed_me = reversed_me + (me // (1 << position)) % 2 * (1 << (levels - 1 - position))
    waves_z = []
    for row in range(depth):
        number = reversed_me + groups * row
        signed = number - total * (number // (total // 2))
        waves_z.append(signed.astype(single) / (total / 2.0))

    def cross(parts, row):
        waves = (wave_x, wave_y, waves_z[row])
        return [
            waves[(c + 1) % 3] * parts[(c + 2) % 3] - waves[(c + 2) % 3] * parts[(c + 1) % 3]
            for c in range(3)
        ]

    def plain_table():
        return table_ref[0], table_ref[1]

    def turned_table():
        return table_ref[2], table_ref[3]

    def gather_blocks(values):
        top, bottom = values[:height], values[height:]
        return jnp.concatenate(
            [
                jnp.concatenate(
                    [
                        top[:, z * breadth : (z + 1) * breadth],
                        bottom[:, z * breadth : (z + 1) * breadth],
                    ],
                    axis=1,
                )
                for z in range(depth)
            ],
            axis=0,
        )

    def spread_blocks(values):
        return jnp.concatenate(
            [
                jnp.concatenate(
                    [
                        values[z * height : (z + 1) * height, p * breadth : (p + 1) * breadth]
                        for z in range(depth)
                    ],
                    axis=1,
                )
                for p in range(2)
            ],
            axis=0,
        )

    def make_planes(b):
        for p in range(2):
            for z in range(depth):
                curls = cross([coeffs_ref[p, c, b, z] for c in range(3)], z)
                for c in range(3):
                    high, low = halves(curls[c])
                    rows, lanes = pl.ds(p * height, height), pl.ds(z * breadth, breadth)
                    high_ref[c, rows, lanes] = high
                    low_ref[c, rows, lanes] = low

        def one(c, carry):
            tall = product(turned_table(), (high_ref[c], low_ref[c]))
            wide = product(halves(gather_blocks(tall)), plain_table())
            for p in range(2):
                for z in range(depth):
                    plane = wide[z * height : (z + 1) * height, p * breadth : (p + 1) * breadth]
                    out1_ref[b, :, c, p, z] = plane.reshape(groups, columns, breadth)
            return carry

        lax.fori_loop(0, 3, one, 0)

    def exchange(out, into, send, recv, b, peer, k):
        return pltpu.make_async_remote_copy(
            src_ref=out.at[b, peer],
            dst_ref=into.at[b, me],
            send_sem=send.at[b, k],
            recv_sem=recv.at[b, k],
            device_id={"gz": peer},
            device_id_type=MESH,
        )

    def arrival(out, into, send, recv, b, source, k):
        return pltpu.make_async_remote_copy(
            src_ref=out.at[b, source],
            dst_ref=into.at[b, source],
            send_sem=send.at[b, k],
            recv_sem=recv.at[b, k],
            device_id={"gz": source},
            device_id_type=MESH,
        )

    def start_all(out, into, send, recv, b):
        each_peer(lambda k, peer, source: exchange(out, into, send, recv, b, peer, k).start())
        into[b, me] = out[b, me]

    def finish_all(out, into, send, recv, b):
        each_peer(
            lambda k, peer, source: arrival(out, into, send, recv, b, source, k).wait_recv()
        )

    def drain_all(out, into, send, recv, b):
        each_peer(lambda k, peer, source: exchange(out, into, send, recv, b, peer, k).wait_send())

    def columns_of(peer):
        return pl.ds(pl.multiple_of(peer * columns, columns), columns)

    def slab_copy(peer, slot, k):
        return pltpu.make_async_remote_copy(
            src_ref=material_ref.at[mine, columns_of(peer), :],
            dst_ref=slab_ref.at[mine, slot],
            send_sem=slab_send.at[k],
            recv_sem=slab_recv.at[k],
            device_id={"gz": peer},
            device_id_type=MESH,
        )

    def half_copy(row):
        return pltpu.make_async_remote_copy(
            src_ref=slab_ref.at[row],
            dst_ref=slab_ref.at[row],
            send_sem=half_sem.at[0],
            recv_sem=half_sem.at[1],
            device_id={"ba": 1 - mine},
            device_id_type=MESH,
        )

    def other_copy(b):
        return pltpu.make_async_remote_copy(
            src_ref=field_ref.at[b],
            dst_ref=other_ref.at[b],
            send_sem=other_send.at[b],
            recv_sem=other_recv.at[b],
            device_id={"ba": 1 - mine},
            device_id_type=MESH,
        )

    loads[0].wait()
    loads[1].wait()
    make_planes(0)
    for load in loads[2:]:
        load.wait()
    pl.semaphore_wait(barrier, groups)
    start_all(out1_ref, in1_ref, send1, recv1, 0)
    each_peer(lambda k, peer, source: slab_copy(peer, me, k).start())
    slab_ref[mine, me] = material_ref[mine, columns_of(me), :]
    for b in range(1, bands):
        make_planes(b)
        start_all(out1_ref, in1_ref, send1, recv1, b)

    each_peer(lambda k, peer, source: slab_copy(source, source, k).wait_recv())
    half_copy(mine).start()
    half_copy(1 - mine).wait_recv()
    kinds = diag_ref.shape[0]
    for row in range(depth):
        codes = slab_ref[row]
        for entry in range(6):
            table = diag_ref if entry < 3 else off_ref
            values = jnp.full(codes.shape, table[0, entry % 3], single)
            for kind in range(1, kinds):
                values = jnp.where(codes == kind, table[kind, entry % 3], values)
            tensor_ref[entry, :, row] = values

    for b in range(bands):
        finish_all(out1_ref, in1_ref, send1, recv1, b)

        def inverse(c, carry):
            points = [
                (in1_ref[b, r // depth, c, 0, r % depth], in1_ref[b, r // depth, c, 1, r % depth])
                for r in range(total)
            ]
            for z, (real, imag) in enumerate(to_voxels(points)):
                field_ref[b, c, 0, z] = real
                field_ref[b, c, 1, z] = imag
            return carry

        lax.fori_loop(0, 3, inverse, 0)
        other_copy(b).start()

        def scale(z, carry):
            xx, yy, zz, xy, yz, zx = [
                tensor_ref[entry, z // depth, z % depth] for entry in range(6)
            ]
            for p in range(2):
                first, second, third = [field_ref[b, c, p, z] for c in range(3)]
                scaled_ref[b, 0, p, z] = xx * first + xy * second + zx * third
                scaled_ref[b, 1, p, z] = xy * first + yy * second + yz * third
                scaled_ref[b, 2, p, z] = zx * first + yz * second + zz * third
            return carry

        lax.fori_loop(0, total, scale, 0, unroll=4)

        def forward(c, carry):
            points = [(scaled_ref[b, c, 0, z], scaled_ref[b, c, 1, z]) for z in range(total)]
            for r, (real, imag) in enumerate(to_waves(points)):
                out2_ref[b, r // depth, c, 0, r % depth] = real
                out2_ref[b, r // depth, c, 1, r % depth] = imag
            return carry

        lax.fori_loop(0, 3, forward, 0)
        start_all(out2_ref, in2_ref, send2, recv2, b)

    def sums_copy(slot, peer, k):
        return pltpu.make_async_remote_copy(
            src_ref=sums_ref.at[slot],
            dst_ref=sums_ref.at[slot],
            send_sem=sums_send.at[k],
            recv_sem=sums_recv.at[k],
            device_id={"gz": peer},
            device_id_type=MESH,
        )

    def make_sums():
        def add(z, sums):
            sums = list(sums)
            for c in range(3):
                ours = [(scaled_ref[b, c, 0, z], scaled_ref[b, c, 1, z]) for b in range(bands)]
                fields = [
                    (source[a, c, 0, z], source[a, c, 1, z])
                    for source in (field_ref, other_ref)
                    for a in range(bands)
                ]
                n = 0
                for t_real, t_imag in ours:
                    for real, imag in fields:
                        sums[n] = sums[n] + (real * t_real + imag * t_imag)
                        sums[n + 1] = sums[n + 1] + (real * t_imag - imag * t_real)
                        n += 2
            return tuple(sums)

        zero = jnp.zeros((columns, breadth), single)
        sums = lax.fori_loop(0, total, add, (zero,) * (4 * bands * bands))
        sums_ref[me] = jnp.concatenate([jnp.sum(v, axis=0, keepdims=True) for v in sums], axis=0)

    half_copy(mine).wait_send()
    each_peer(lambda k, peer, source: slab_copy(peer, me, k).wait_send())
    for b in range(bands):
        drain_all(out1_ref, in1_ref, send1, recv1, b)

    for b in range(bands):
        if b == bands - 1:
            for a in range(bands):
                other_copy(a).wait_send()
                other_copy(a).wait_recv()
            make_sums()
            each_peer(lambda k, peer, source: sums_copy(me, peer, k).start())
            for a in range(b):
                drain_all(out2_ref, in2_ref, send2, recv2, a)
        finish_all(out2_ref, in2_ref, send2, recv2, b)

        def plane_of(c, carry):
            planes = jnp.concatenate(
                [
                    jnp.concatenate(
                        [in2_ref[b, :, c, p, z].reshape(height, breadth) for p in range(2)], axis=1
                    )
                    for z in range(depth)
                ],
                axis=0,
            )
            wide = product(halves(planes), turned_table())
            back_ref[c] = product(plain_table(), halves(spread_blocks(wide)))
            return carry

        lax.fori_loop(0, 3, plane_of, 0)

        for z in range(depth):
            for p in range(2):
                rows, lanes = pl.ds(p * height, height), pl.ds(z * breadth, breadth)
                crossed = cross([back_ref[c, rows, lanes] for c in range(3)], z)
                for c in range(3):
                    theta_ref[p, c, b, z] = -crossed[c]

    drain_all(out2_ref, in2_ref, send2, recv2, bands - 1)
    each_peer(lambda k, peer, source: sums_copy(source, source, k).wait_recv())
    gram_ref[...] = jnp.sum(sums_ref[...], axis=0)
    each_peer(lambda k, peer, source: sums_copy(me, peer, k).wait_send())


def on_device_kernel(coeffs, material, inv_diag, inv_off):
    groups = lax.axis_size("gz")
    _, comps, bands, depth, height, breadth = coeffs.shape
    total = depth * groups
    columns = height // groups
    table = jnp.asarray(split_table(breadth, total**-0.25))
    grams = bands * 4 * bands
    voxels = (bands, 3, 2, total, columns, breadth)
    block = (bands, groups, 3, 2, depth, columns, breadth)
    vmem = pl.BlockSpec(memory_space=pltpu.VMEM)
    hbm = pl.BlockSpec(memory_space=pltpu.HBM)
    dma = pltpu.SemaphoreType.DMA
    theta, sums = pl.pallas_call(
        functools.partial(operator_kernel, groups),
        out_shape=(
            jax.ShapeDtypeStruct(coeffs.shape, single),
            jax.ShapeDtypeStruct((grams, breadth), single),
        ),
        in_specs=[hbm, hbm, hbm, hbm, hbm],
        out_specs=(vmem, vmem),
        scratch_shapes=[
            pltpu.VMEM(coeffs.shape, single),
            pltpu.VMEM(material.shape, jnp.int32),
            pltpu.VMEM(table.shape, half),
            pltpu.SMEM(inv_diag.shape, single),
            pltpu.SMEM(inv_off.shape, single),
            pltpu.VMEM((depth, groups, columns, breadth), jnp.int32),
            pltpu.VMEM((6, groups, depth, columns, breadth), single),
            pltpu.VMEM((3, 2 * height, depth * breadth), half),
            pltpu.VMEM((3, 2 * height, depth * breadth), half),
            pltpu.VMEM((3, 2 * height, depth * breadth), single),
            pltpu.VMEM(voxels, single),
            pltpu.VMEM(voxels, single),
            pltpu.VMEM(voxels, single),
            pltpu.VMEM(block, single),
            pltpu.VMEM(block, single),
            pltpu.VMEM(block, single),
            pltpu.VMEM(block, single),
            pltpu.VMEM((groups, grams, breadth), single),
            dma((5,)),
            dma((groups,)),
            dma((groups,)),
            dma((2,)),
            dma((bands, groups)),
            dma((bands, groups)),
            dma((bands, groups)),
            dma((bands, groups)),
            dma((bands,)),
            dma((bands,)),
            dma((groups,)),
            dma((groups,)),
        ],
        compiler_params=pltpu.CompilerParams(
            collective_id=0, has_side_effects=True, vmem_limit_bytes=48 * 1024 * 1024
        ),
        name="maxwell",
    )(coeffs, material, inv_diag, inv_off, table)
    values = jnp.sum(sums, axis=1) / (breadth * height * total)
    values = values.reshape(bands, 2, bands, 2).transpose(1, 3, 2, 0)
    own, other = values[0], values[1]
    first = lax.axis_index("ba") == 0
    gram = jnp.concatenate([jnp.where(first, own, other), jnp.where(first, other, own)], axis=1)
    return (theta, gram)


def fits(coeffs):
    groups, depth, height, breadth = (
        lax.axis_size("gz"),
        coeffs.shape[3],
        coeffs.shape[4],
        coeffs.shape[5],
    )
    return (
        lax.axis_size("ba") == 2
        and depth == 2
        and height % (8 * groups) == 0
        and height == breadth
        and breadth % 128 == 0
    )


def on_either(coeffs, material, inv_diag, inv_off):
    chosen = on_device_kernel if fits(coeffs) else on_device
    return chosen(coeffs, material, inv_diag, inv_off)


def solution(mesh):
    in_specs = (P(None, None, "ba", "gz", None, None), P("gz", None, None), P(), P())
    out_specs = (P(None, None, "ba", "gz", None, None), P(None, None, "ba"))
    return jax.shard_map(
        on_either, mesh=mesh, in_specs=in_specs, out_specs=out_specs, check_vma=False
    )
```

profile of v0, /device:TPU:0, one launch (start us, length us, event | category | flops | bytes accessed | tf_op | source)
XLA Modules:
  0.0 89.6 jit_solution(490699706279845306)
XLA Ops:
  0.6 0.0 copy-start
  0.6 1.4 %copy-done = f32[2,3,2,2,128,128]{5,4,3,2,1,0:T(8,128)S(1)} copy-done((f32[2,3,2,2,128,128]{5,4,3,2,1,0:T(8,128)S(1)}, f32[2,3,2,2,128,128]{5,4,3,2,1,0:T(8,128)}, u32[]{:S(2)}) %copy-start) | copy-done | bytes 1572888
  2.0 0.0 copy-start.1
  2.0 1.0 %copy-done.1 = bf16[4,256,256]{2,1,0:T(8,128)(2,1)S(1)} copy-done((bf16[4,256,256]{2,1,0:T(8,128)(2,1)S(1)}, bf16[4,256,256]{2,1,0:T(8,128)(2,1)}, u32[]{:S(2)}) %copy-start.1) | copy-done | bytes 524312
  3.1 0.0 copy-start.2
  3.1 0.9 %copy-done.2 = s32[2,128,128]{2,1,0:T(8,128)S(1)} copy-done((s32[2,128,128]{2,1,0:T(8,128)S(1)}, s32[2,128,128]{2,1,0:T(8,128)}, u32[]{:S(2)}) %copy-start.2) | copy-done | bytes 131096
  4.0 0.0 copy-start.3
  4.0 0.7 copy-done.3
  4.7 0.0 copy-start.4
  4.7 0.7 copy-done.4
  5.4 82.0 %maxwell.1 = (f32[2,3,2,2,128,128]{5,4,3,2,1,0:T(8,128)S(1)}, f32[16,128]{1,0:T(8,128)S(1)}) custom-call(f32[2,3,2,2,128,128]{5,4,3,2,1,0:T(8,128)S(1)} %copy-done, s32[2,128,128]{2,1,0:T(8,128)S(1)} %copy-done.2, f32[4,3]{1,0:T(4,128)S(1)} %copy-done.3, f32[4,3]{1,0:T(4,128)S(1)} %copy-done.4, bf16[4,256,256]{2,1,0:T(8,128)(2,1)S(1)} %copy-done.1), custom_call_target="tpu_custom_call" | custom-call | tf_op jit(solution)/shard_map/maxwell/pallas_call | solution.py:589
  87.4 0.1 reduce_sum.9
  87.5 0.1 div.6
  87.6 0.1 copy.7
  87.7 0.1 copy.8
  87.8 0.7 copy.9
  88.5 1.1 %copy.11 = f32[2,3,2,2,128,128]{5,4,3,2,1,0:T(8,128)} copy(f32[2,3,2,2,128,128]{5,4,3,2,1,0:T(8,128)S(1)} %get-tuple-element.12) | data formatting | bytes 3145728
  (3 shorter events, 0.0 us)
Async XLA Ops:
  0.6 1.4 %copy-start = (f32[2,3,2,2,128,128]{5,4,3,2,1,0:T(8,128)S(1)}, f32[2,3,2,2,128,128]{5,4,3,2,1,0:T(8,128)}, u32[]{:S(2)}) copy-start(f32[2,3,2,2,128,128]{5,4,3,2,1,0:T(8,128)} %coeffs_hbm.1) | copy-start | bytes 4718596
  2.0 1.0 %copy-start.1 = (bf16[4,256,256]{2,1,0:T(8,128)(2,1)S(1)}, bf16[4,256,256]{2,1,0:T(8,128)(2,1)}, u32[]{:S(2)}) copy-start(bf16[4,256,256]{2,1,0:T(8,128)(2,1)} %constant.13.clone.table_hbm) | copy-start | bytes 1572868
  3.1 0.9 %copy-start.2 = (s32[2,128,128]{2,1,0:T(8,128)S(1)}, s32[2,128,128]{2,1,0:T(8,128)}, u32[]{:S(2)}) copy-start(s32[2,128,128]{2,1,0:T(8,128)} %material_hbm.1) | copy-start | bytes 393220
  4.0 0.7 copy-start.3
  4.7 0.7 copy-start.4
where the time goes:
time: 89.9 us; the launch traced here: 89.6 us
  Pallas kernels  82 us (91%)
  local copies, waits for them, and re-layouts  6.82 us (8%)
    pallas_call x1, Pallas kernels, on_device_kernel(): pl.pallas_call(functools.partial(operator_kernel, groups), out_shape=(jax...  82 us
    unnamed x12, local copies, waits for them, and re-layouts  6.53 us

commit v1 on v0

--- a/solution.py
+++ b/solution.py
@@ -627,7 +627,7 @@
             dma((groups,)),
         ],
         compiler_params=pltpu.CompilerParams(
-            collective_id=0, has_side_effects=True, vmem_limit_bytes=48 * 1024 * 1024
+            collective_id=0, has_side_effects=True, vmem_limit_bytes=56 * 1024 * 1024
         ),
         name="maxwell",
     )(coeffs, material, inv_diag, inv_off, table)

time: 89.9 us -> 89.8 us (level)
  local copies, waits for them, and re-layouts: 6.82 us -> 3.67 us
  Pallas kernels: 82 us -> 84.4 us
    unnamed x12 -> x2, local copies, waits for them, and re-layouts: 6.53 us -> 3.38 us
    pallas_call x1, Pallas kernels: 82 us -> 84.4 us  [on_device_kernel(): pl.pallas_call(functools.partial(operator_kernel, groups), out_shape=(jax...]
where the time goes in v1:
time: 89.8 us; the launch traced here: 89.6 us
  Pallas kernels  84.4 us (94%)
  local copies, waits for them, and re-layouts  3.67 us (4%)
    pallas_call x1, Pallas kernels, on_device_kernel(): pl.pallas_call(functools.partial(operator_kernel, groups), out_shape=(jax...  84.4 us
    unnamed x2, local copies, waits for them, and re-layouts  3.38 us

profile of v1, /device:TPU:0, one launch (start us, length us, event | category | flops | bytes accessed | tf_op | source)
XLA Modules:
  0.0 89.6 jit_solution(4587925773608009788)
XLA Ops:
  0.6 84.4 %maxwell.1 = (f32[2,3,2,2,128,128]{5,4,3,2,1,0:T(8,128)}, f32[16,128]{1,0:T(8,128)}) custom-call(f32[2,3,2,2,128,128]{5,4,3,2,1,0:T(8,128)} %coeffs_hbm.1, s32[2,128,128]{2,1,0:T(8,128)} %material_hbm.1, f32[4,3]{1,0:T(4,128)} %diag_hbm.1, f32[4,3]{1,0:T(4,128)} %off_hbm.1, bf16[4,256,256]{2,1,0:T(8,128)(2,1)} %constant.13.clone.table_hbm), custom_call_target="tpu_custom_call" | custom-call | tf_op jit(solution)/shard_map/maxwell/pallas_call | solution.py:589
  85.1 0.8 reduce_sum.9
  85.9 0.1 div.6
  86.0 0.1 copy.7
  86.1 0.1 copy.8
  86.2 0.7 copy.9
  86.9 2.7 %copy.11 = f32[2,3,2,2,128,128]{5,4,3,2,1,0:T(8,128)} copy(f32[2,3,2,2,128,128]{5,4,3,2,1,0:T(8,128)} %get-tuple-element.12) | data formatting | bytes 3145728
  (3 shorter events, 0.0 us)

commit v2 on v0

--- a/solution.py
+++ b/solution.py
@@ -586,6 +586,7 @@
     vmem = pl.BlockSpec(memory_space=pltpu.VMEM)
     hbm = pl.BlockSpec(memory_space=pltpu.HBM)
     dma = pltpu.SemaphoreType.DMA
+    coeffs, material, inv_diag, inv_off, table = [pltpu.with_memory_space_constraint(v, pltpu.HBM) for v in (coeffs, material, inv_diag, inv_off, table)]
     theta, sums = pl.pallas_call(
         functools.partial(operator_kernel, groups),
         out_shape=(

time: 89.9 us -> 86.3 us (0.960)
  local copies, waits for them, and re-layouts: 6.82 us -> 2.11 us
  Pallas kernels: 82 us -> 83.3 us
    unnamed x12 -> x2, local copies, waits for them, and re-layouts: 6.53 us -> 1.82 us
    pallas_call x1, Pallas kernels: 82 us -> 83.3 us  [on_device_kernel(): pl.pallas_call(functools.partial(operator_kernel, groups), out_shape=(jax...]
where the time goes in v2:
time: 86.3 us; the launch traced here: 86.2 us
  Pallas kernels  83.3 us (97%)
  local copies, waits for them, and re-layouts  2.11 us (2%)
    pallas_call x1, Pallas kernels, on_device_kernel(): pl.pallas_call(functools.partial(operator_kernel, groups), out_shape=(jax...  83.3 us
    unnamed x2, local copies, waits for them, and re-layouts  1.82 us

profile of v2, /device:TPU:0, one launch (start us, length us, event | category | flops | bytes accessed | tf_op | source)
XLA Modules:
  0.0 86.2 jit_solution(3455751602586566336)
XLA Ops:
  0.6 83.3 %maxwell.1 = (f32[2,3,2,2,128,128]{5,4,3,2,1,0:T(8,128)S(1)}, f32[16,128]{1,0:T(8,128)S(1)}) custom-call(f32[2,3,2,2,128,128]{5,4,3,2,1,0:T(8,128)} %coeffs_hbm.1, s32[2,128,128]{2,1,0:T(8,128)} %material_hbm.1, f32[4,3]{1,0:T(4,128)} %diag_hbm.1, f32[4,3]{1,0:T(4,128)} %off_hbm.1, bf16[4,256,256]{2,1,0:T(8,128)(2,1)} %constant.13.clone.table_hbm), custom_call_target="tpu_custom_call" | custom-call | tf_op jit(solution)/shard_map/maxwell/pallas_call | solution.py:590
  83.9 0.1 reduce_sum.9
  84.0 0.1 div.6
  84.1 0.1 copy.7
  84.2 0.1 copy.8
  84.3 0.7 copy.9
  85.0 1.1 %copy.11 = f32[2,3,2,2,128,128]{5,4,3,2,1,0:T(8,128)} copy(f32[2,3,2,2,128,128]{5,4,3,2,1,0:T(8,128)S(1)} %get-tuple-element.12) | data formatting | bytes 3145728
  (3 shorter events, 0.0 us)

commit v3 on v0

--- a/solution.py
+++ b/solution.py
@@ -226,11 +226,15 @@
     high_ref,
     low_ref,
     back_ref,
+    pair_ref,
+    other_ref,
+    swap_ref,
+    result_ref,
+    return_ref,
+    out1_ref,
+    in1_ref,
     field_ref,
     scaled_ref,
-    other_ref,
-    out1_ref,
-    in1_ref,
     out2_ref,
     in2_ref,
     sums_ref,
@@ -242,6 +246,10 @@
     recv1,
     send2,
     recv2,
+    swap_send,
+    swap_recv,
+    return_send,
+    return_recv,
     other_send,
     other_recv,
     sums_send,
@@ -249,23 +257,31 @@
 ):
     _, comps, bands, depth, height, breadth = coeffs_ref.shape
     total = depth * groups
-    columns = height // groups
+    members = groups // 2
+    columns = height // members
     levels = groups.bit_length() - 1
     me = lax.axis_index("gz")
     mine = lax.axis_index("ba")
-    middle = groups // 2
-
-    def offset_of(i):
-        away = (i + 1) // 2
-        return middle + away - 2 * away * (i % 2)
+    side = me // members
+    seat = me % members
+    partner = (me + members) % groups
+    mate = {"ba": 1 - mine}
+    step_rows = 16
+    steps = height // step_rows
 
     def each_peer(body):
-        def step(i, carry):
-            k = offset_of(i)
+        def step(k, carry):
             body(k, (me + k) % groups, (me + groups - k) % groups)
             return carry
 
-        lax.fori_loop(0, groups - 1, step, 0)
+        lax.fori_loop(1, groups, step, 0)
+
+    def each_member(body):
+        def step(k, carry):
+            body(k, (seat + k) % members, (seat + members - k) % members)
+            return carry
+
+        lax.fori_loop(1, members, step, 0)
 
     barrier = pltpu.get_barrier_semaphore()
     each_peer(
@@ -273,41 +289,129 @@
             barrier, inc=1, device_id={"gz": peer}, device_id_type=MESH
         )
     )
-    pl.semaphore_signal(barrier, inc=1, device_id={"ba": 1 - mine}, device_id_type=MESH)
+    pl.semaphore_signal(barrier, inc=1, device_id=mate, device_id_type=MESH)
+
+    def band_load(b, n):
+        return pltpu.make_async_copy(
+            coeffs_hbm.at[:, :, b], coeffs_ref.at[:, :, b], load_sem.at[n]
+        )
 
     loads = [
-        pltpu.make_async_copy(coeffs_hbm, coeffs_ref, load_sem.at[0]),
-        pltpu.make_async_copy(table_hbm, table_ref, load_sem.at[1]),
-        pltpu.make_async_copy(material_hbm, material_ref, load_sem.at[2]),
-        pltpu.make_async_copy(diag_hbm, diag_ref, load_sem.at[3]),
-        pltpu.make_async_copy(off_hbm, off_ref, load_sem.at[4]),
+        band_load(1 - side, 0),
+        band_load(side, 1),
+        pltpu.make_async_copy(table_hbm, table_ref, load_sem.at[2]),
+        pltpu.make_async_copy(material_hbm, material_ref, load_sem.at[3]),
+        pltpu.make_async_copy(diag_hbm, diag_ref, load_sem.at[4]),
+        pltpu.make_async_copy(off_hbm, off_ref, load_sem.at[5]),
     ]
     for load in loads:
         load.start()
 
-    across = lax.broadcasted_iota(jnp.int32, (1, breadth), 1)
-    upward = lax.broadcasted_iota(jnp.int32, (height, 1), 0)
-    wave_x = jnp.where(across < breadth // 2, across, across - breadth).astype(single) / (
-        breadth / 2.0
-    )
-    wave_y = jnp.where(upward < height // 2, upward, upward - height).astype(single) / (
-        height / 2.0
-    )
-    reversed_me = 0
-    for position in range(levels):
-        reversed_me = reversed_me + (me // (1 << position)) % 2 * (1 << (levels - 1 - position))
-    waves_z = []
-    for row in range(depth):
-        number = reversed_me + groups * row
-        signed = number - total * (number // (total // 2))
-        waves_z.append(signed.astype(single) / (total / 2.0))
-
-    def cross(parts, row):
-        waves = (wave_x, wave_y, waves_z[row])
-        return [
-            waves[(c + 1) % 3] * parts[(c + 2) % 3] - waves[(c + 2) % 3] * parts[(c + 1) % 3]
-            for c in range(3)
-        ]
+    def signed(number, length):
+        return number - length * (number // (length // 2))
+
+    def row_number(owner, row):
+        reversed_owner = 0
+        for position in range(levels):
+            bit = (owner // (1 << position)) % 2
+            reversed_owner = reversed_owner + bit * (1 << (levels - 1 - position))
+        return signed(reversed_owner + groups * row, total)
+
+    def inverse_of(values):
+        zero = values == 0
+        return jnp.where(zero, 0.0, 1.0 / jnp.where(zero, 1, values).astype(single))
+
+    class Waves:
+        def __init__(self, owner, row, i):
+            shape = (step_rows, breadth)
+            nx = lax.broadcasted_iota(jnp.int32, shape, 1)
+            ny = lax.broadcasted_iota(jnp.int32, shape, 0) + i * step_rows
+            nx = jnp.where(nx < breadth // 2, nx, nx - breadth)
+            ny = jnp.where(ny < height // 2, ny, ny - height)
+            nz = jnp.full(shape, row_number(owner, row), jnp.int32)
+            self.x = nx.astype(single) / (breadth / 2.0)
+            self.y = ny.astype(single) / (height / 2.0)
+            self.z = nz.astype(single) / (total / 2.0)
+            ax, ay, az = jnp.abs(nx) * total, jnp.abs(ny) * total, jnp.abs(nz) * breadth
+            self.is_x = (ax >= ay) & (ax >= az)
+            self.is_y = ay >= az
+            self.numbers = (nx, ny, nz)
+
+        def cross(self, v):
+            q = (self.x, self.y, self.z)
+            return [
+                q[(c + 1) % 3] * v[(c + 2) % 3] - q[(c + 2) % 3] * v[(c + 1) % 3]
+                for c in range(3)
+            ]
+
+        def pick(self, first, second, third):
+            return jnp.where(self.is_x, first, jnp.where(self.is_y, second, third))
+
+        def inverse(self):
+            nx, ny, nz = self.numbers
+            scaled = self.pick(nx * total, ny * total, nz * breadth)
+            return inverse_of(scaled) * (total * breadth / 2.0)
+
+        def ratios(self):
+            inverse = self.inverse()
+            return (
+                self.pick(self.y, self.z, self.x) * inverse,
+                self.pick(self.z, self.x, self.y) * inverse,
+            )
+
+        def reduce(self, v):
+            return self.pick(v[1], v[2], v[0]), self.pick(v[2], v[0], v[1])
+
+        def rebuild(self, ratios, first, second):
+            last = -(ratios[0] * first + ratios[1] * second)
+            return [
+                self.pick(last, second, first),
+                self.pick(first, last, second),
+                self.pick(second, first, last),
+            ]
+
+    def rows_of(i):
+        return pl.ds(pl.multiple_of(i * step_rows, step_rows), step_rows)
+
+    def each_step(body):
+        def step(n, carry):
+            body(n // steps, n % steps)
+            return carry
+
+        lax.fori_loop(0, depth * steps, step, 0)
+
+    def put_halves(curls, p, row, i):
+        at = pl.ds(pl.multiple_of(p * height + i * step_rows, step_rows), step_rows)
+        lanes = pl.ds(pl.multiple_of(row * breadth, breadth), breadth)
+        for c in range(3):
+            high, low = halves(curls[c])
+            high_ref[c, at, lanes] = high
+            low_ref[c, at, lanes] = low
+
+    def put_pair(b, p, row, i, pair):
+        for n in range(2):
+            pair_ref[b, row, n, p, rows_of(i), :] = pair[n]
+
+    def away_step(row, i):
+        waves = Waves(me, row, i)
+        for p in range(2):
+            values = [coeffs_ref[p, c, 1 - side, row, rows_of(i), :] for c in range(3)]
+            put_pair(1 - side, p, row, i, waves.reduce(waves.cross(values)))
+
+    def home_step(row, i):
+        waves = Waves(me, row, i)
+        for p in range(2):
+            values = [coeffs_ref[p, c, side, row, rows_of(i), :] for c in range(3)]
+            curls = waves.cross(values)
+            put_halves(curls, p, row, i)
+            put_pair(side, p, row, i, waves.reduce(curls))
+
+    def guest_step(row, i):
+        waves = Waves(partner, row, i)
+        ratios = waves.ratios()
+        for p in range(2):
+            pair = [swap_ref[row, n, p, rows_of(i), :] for n in range(2)]
+            put_halves(waves.rebuild(ratios, *pair), p, row, i)
 
     def plain_table():
         return table_ref[0], table_ref[1]
@@ -346,61 +450,102 @@
             axis=0,
         )
 
-    def make_planes(b):
-        for p in range(2):
-            for z in range(depth):
-                curls = cross([coeffs_ref[p, c, b, z] for c in range(3)], z)
-                for c in range(3):
-                    high, low = halves(curls[c])
-                    rows, lanes = pl.ds(p * height, height), pl.ds(z * breadth, breadth)
-                    high_ref[c, rows, lanes] = high
-                    low_ref[c, rows, lanes] = low
-
+    def to_peer(out, into, send, recv, s, c, k, peer, from_at, to_at):
+        return pltpu.make_async_remote_copy(
+            src_ref=out.at[from_at, peer, c],
+            dst_ref=into.at[to_at, seat, c],
+            send_sem=send.at[s, c, k],
+            recv_sem=recv.at[s, c, k],
+            device_id={"gz": side * members + peer},
+            device_id_type=MESH,
+        )
+
+    def from_peer(out, into, send, recv, s, c, k, source, from_at, to_at):
+        return pltpu.make_async_remote_copy(
+            src_ref=out.at[from_at, source, c],
+            dst_ref=into.at[to_at, source, c],
+            send_sem=send.at[s, c, k],
+            recv_sem=recv.at[s, c, k],
+            device_id={"gz": side * members + source},
+            device_id_type=MESH,
+        )
+
+    def ends1(s):
+        return s, (side + s) % 2
+
+    def ends2(s):
+        return (side + s) % 2, s
+
+    def start_all(out, into, send, recv, s, c, ends):
+        each_member(
+            lambda k, peer, source: to_peer(
+                out, into, send, recv, s, c, k, peer, *ends
+            ).start()
+        )
+        into[ends[1], seat, c] = out[ends[0], seat, c]
+
+    def finish_all(out, into, send, recv, s, c, ends):
+        each_member(
+            lambda k, peer, source: from_peer(
+                out, into, send, recv, s, c, k, source, *ends
+            ).wait_recv()
+        )
+
+    def drain_all(out, into, send, recv, s, c, ends):
+        each_member(
+            lambda k, peer, source: to_peer(
+                out, into, send, recv, s, c, k, peer, *ends
+            ).wait_send()
+        )
+
+    first = (out1_ref, in1_ref, send1, recv1)
+    second = (out2_ref, in2_ref, send2, recv2)
+
+    def make_planes(s):
         def one(c, carry):
             tall = product(turned_table(), (high_ref[c], low_ref[c]))
             wide = product(halves(gather_blocks(tall)), plain_table())
             for p in range(2):
                 for z in range(depth):
                     plane = wide[z * height : (z + 1) * height, p * breadth : (p + 1) * breadth]
-                    out1_ref[b, :, c, p, z] = plane.reshape(groups, columns, breadth)
+                    out1_ref[s, :, c, p, z] = plane.reshape(members, columns, breadth)
+            start_all(*first, s, c, ends1(s))
             return carry
 
         lax.fori_loop(0, 3, one, 0)
 
-    def exchange(out, into, send, recv, b, peer, k):
+    def swap_copy(row):
         return pltpu.make_async_remote_copy(
-            src_ref=out.at[b, peer],
-            dst_ref=into.at[b, me],
-            send_sem=send.at[b, k],
-            recv_sem=recv.at[b, k],
-            device_id={"gz": peer},
+            src_ref=pair_ref.at[1 - side, row],
+            dst_ref=swap_ref.at[row],
+            send_sem=swap_send.at[row],
+            recv_sem=swap_recv.at[row],
+            device_id={"gz": partner},
             device_id_type=MESH,
         )
 
-    def arrival(out, into, send, recv, b, source, k):
+    def return_copy(row):
         return pltpu.make_async_remote_copy(
-            src_ref=out.at[b, source],
-            dst_ref=into.at[b, source],
-            send_sem=send.at[b, k],
-            recv_sem=recv.at[b, k],
-            device_id={"gz": source},
+            src_ref=result_ref.at[row],
+            dst_ref=return_ref.at[row],
+            send_sem=return_send.at[row],
+            recv_sem=return_recv.at[row],
+            device_id={"gz": partner},
             device_id_type=MESH,
         )
 
-    def start_all(out, into, send, recv, b):
-        each_peer(lambda k, peer, source: exchange(out, into, send, recv, b, peer, k).start())
-        into[b, me] = out[b, me]
-
-    def finish_all(out, into, send, recv, b):
-        each_peer(
-            lambda k, peer, source: arrival(out, into, send, recv, b, source, k).wait_recv()
-        )
-
-    def drain_all(out, into, send, recv, b):
-        each_peer(lambda k, peer, source: exchange(out, into, send, recv, b, peer, k).wait_send())
+    def other_copy(b, n):
+        return pltpu.make_async_remote_copy(
+            src_ref=pair_ref.at[b],
+            dst_ref=other_ref.at[b],
+            send_sem=other_send.at[n],
+            recv_sem=other_recv.at[n],
+            device_id=mate,
+            device_id_type=MESH,
+        )
 
     def columns_of(peer):
-        return pl.ds(pl.multiple_of(peer * columns, columns), columns)
+        return pl.ds(pl.multiple_of((peer % members) * columns, columns), columns)
 
     def slab_copy(peer, slot, k):
         return pltpu.make_async_remote_copy(
@@ -418,84 +563,188 @@
             dst_ref=slab_ref.at[row],
             send_sem=half_sem.at[0],
             recv_sem=half_sem.at[1],
-            device_id={"ba": 1 - mine},
+            device_id=mate,
             device_id_type=MESH,
         )
 
-    def other_copy(b):
-        return pltpu.make_async_remote_copy(
-            src_ref=field_ref.at[b],
-            dst_ref=other_ref.at[b],
-            send_sem=other_send.at[b],
-            recv_sem=other_recv.at[b],
-            device_id={"ba": 1 - mine},
-            device_id_type=MESH,
-        )
-
     loads[0].wait()
+    each_step(away_step)
+    pl.semaphore_wait(barrier, groups)
+    swap_copy(0).start()
+    other_copy(1 - side, 0).start()
     loads[1].wait()
+    each_step(home_step)
+    other_copy(side, 1).start()
+    loads[2].wait()
     make_planes(0)
-    for load in loads[2:]:
+    swap_copy(1).start()
+    for load in loads[3:]:
         load.wait()
-    pl.semaphore_wait(barrier, groups)
-    start_all(out1_ref, in1_ref, send1, recv1, 0)
     each_peer(lambda k, peer, source: slab_copy(peer, me, k).start())
     slab_ref[mine, me] = material_ref[mine, columns_of(me), :]
-    for b in range(1, bands):
-        make_planes(b)
-        start_all(out1_ref, in1_ref, send1, recv1, b)
+
+    for row in range(depth):
+        swap_copy(row).wait_recv()
+    each_step(guest_step)
+    make_planes(1)
 
     each_peer(lambda k, peer, source: slab_copy(source, source, k).wait_recv())
     half_copy(mine).start()
     half_copy(1 - mine).wait_recv()
     kinds = diag_ref.shape[0]
-    for row in range(depth):
-        codes = slab_ref[row]
-        for entry in range(6):
-            table = diag_ref if entry < 3 else off_ref
-            values = jnp.full(codes.shape, table[0, entry % 3], single)
-            for kind in range(1, kinds):
-                values = jnp.where(codes == kind, table[kind, entry % 3], values)
-            tensor_ref[entry, :, row] = values
-
-    for b in range(bands):
-        finish_all(out1_ref, in1_ref, send1, recv1, b)
-
-        def inverse(c, carry):
+
+    def tensor_step(owner, carry):
+        for row in range(depth):
+            codes = slab_ref[row, owner]
+            for entry in range(6):
+                table = diag_ref if entry < 3 else off_ref
+                values = jnp.full(codes.shape, table[0, entry % 3], single)
+                for kind in range(1, kinds):
+                    values = jnp.where(codes == kind, table[kind, entry % 3], values)
+                tensor_ref[entry, owner, row] = values
+        return carry
+
+    lax.fori_loop(0, groups, tensor_step, 0)
+
+    def part_of(n):
+        return pl.ds(pl.multiple_of(n * 8, 8), 8)
+
+    def inverse(c, carry):
+        for s in range(2):
+            finish_all(*first, s, c, ends1(s))
+
+        def part(n, carry):
+            points = []
+            for r in range(total):
+                owner, row = r // depth, r % depth
+                at = (owner // members, owner % members, c)
+                points.append(
+                    (in1_ref[(*at, 0, row, part_of(n))], in1_ref[(*at, 1, row, part_of(n))])
+                )
+            for z, (real, imag) in enumerate(to_voxels(points)):
+                field_ref[c, 0, z, part_of(n)] = real
+                field_ref[c, 1, z, part_of(n)] = imag
+            return carry
+
+        return lax.fori_loop(0, columns // 8, part, carry)
+
+    lax.fori_loop(0, 3, inverse, 0)
+
+    def scale(z, carry):
+        xx, yy, zz, xy, yz, zx = [tensor_ref[entry, z // depth, z % depth] for entry in range(6)]
+        for p in range(2):
+            fx, fy, fz = [field_ref[c, p, z] for c in range(3)]
+            scaled_ref[0, p, z] = xx * fx + xy * fy + zx * fz
+            scaled_ref[1, p, z] = xy * fx + yy * fy + yz * fz
+            scaled_ref[2, p, z] = zx * fx + yz * fy + zz * fz
+        return carry
+
+    lax.fori_loop(0, total, scale, 0, unroll=2)
+
+    def forward(c, carry):
+        def part(n, carry):
             points = [
-                (in1_ref[b, r // depth, c, 0, r % depth], in1_ref[b, r // depth, c, 1, r % depth])
-                for r in range(total)
+                (scaled_ref[c, 0, z, part_of(n)], scaled_ref[c, 1, z, part_of(n)])
+                for z in range(total)
             ]
-            for z, (real, imag) in enumerate(to_voxels(points)):
-                field_ref[b, c, 0, z] = real
-                field_ref[b, c, 1, z] = imag
+            for r, (real, imag) in enumerate(to_waves(points)):
+                owner, row = r // depth, r % depth
+                at = (owner // members, owner % members, c)
+                out2_ref[(*at, 0, row, part_of(n))] = real
+                out2_ref[(*at, 1, row, part_of(n))] = imag
             return carry
 
-        lax.fori_loop(0, 3, inverse, 0)
-        other_copy(b).start()
-
-        def scale(z, carry):
-            xx, yy, zz, xy, yz, zx = [
-                tensor_ref[entry, z // depth, z % depth] for entry in range(6)
-            ]
-            for p in range(2):
-                first, second, third = [field_ref[b, c, p, z] for c in range(3)]
-                scaled_ref[b, 0, p, z] = xx * first + xy * second + zx * third
-                scaled_ref[b, 1, p, z] = xy * first + yy * second + yz * third
-                scaled_ref[b, 2, p, z] = zx * first + yz * second + zz * third
+        lax.fori_loop(0, columns // 8, part, 0)
+        start_all(*second, 1, c, ends2(1))
+        return carry
+
+    lax.fori_loop(0, 3, forward, 0)
+
+    def start_home(c, carry):
+        start_all(*second, 0, c, ends2(0))
+        return carry
+
+    lax.fori_loop(0, 3, start_home, 0)
+
+    def take_planes(s):
+        def one(c, carry):
+            finish_all(*second, s, c, ends2(s))
+            planes = jnp.concatenate(
+                [
+                    jnp.concatenate(
+                        [in2_ref[s, :, c, p, z].reshape(height, breadth) for p in range(2)], axis=1
+                    )
+                    for z in range(depth)
+                ],
+                axis=0,
+            )
+            wide = product(halves(planes), turned_table())
+            back_ref[c] = product(plain_table(), halves(spread_blocks(wide)))
             return carry
 
-        lax.fori_loop(0, total, scale, 0, unroll=4)
-
-        def forward(c, carry):
-            points = [(scaled_ref[b, c, 0, z], scaled_ref[b, c, 1, z]) for z in range(total)]
-            for r, (real, imag) in enumerate(to_waves(points)):
-                out2_ref[b, r // depth, c, 0, r % depth] = real
-                out2_ref[b, r // depth, c, 1, r % depth] = imag
-            return carry
-
-        lax.fori_loop(0, 3, forward, 0)
-        start_all(out2_ref, in2_ref, send2, recv2, b)
+        lax.fori_loop(0, 3, one, 0)
+
+    def theta_at(waves, p, row, i):
+        at = pl.ds(pl.multiple_of(p * height + i * step_rows, step_rows), step_rows)
+        lanes = pl.ds(pl.multiple_of(row * breadth, breadth), breadth)
+        return [-v for v in waves.cross([back_ref[c, at, lanes] for c in range(3)])]
+
+    def guest_result(row, i):
+        waves = Waves(partner, row, i)
+        for p in range(2):
+            pair = waves.reduce(theta_at(waves, p, row, i))
+            for n in range(2):
+                result_ref[row, n, p, rows_of(i), :] = pair[n]
+
+    def add_sums(waves, pairs, row, i, sums):
+        inverse = waves.inverse()
+        (real1, real2), (imag1, imag2) = [[inverse * v for v in pair] for pair in pairs]
+        sums = list(sums)
+        n = 0
+        for source in (pair_ref, other_ref):
+            for a in range(bands):
+                one_real, one_imag = [source[a, row, 0, p, rows_of(i), :] for p in range(2)]
+                two_real, two_imag = [source[a, row, 1, p, rows_of(i), :] for p in range(2)]
+                real = (two_real * real1 + two_imag * imag1) - (one_real * real2 + one_imag * imag2)
+                imag = (two_real * imag1 - two_imag * real1) - (one_real * imag2 - one_imag * real2)
+                sums[n] = sums[n] + real
+                sums[n + 1] = sums[n + 1] + imag
+                n += 2
+        return tuple(sums)
+
+    def each_sum(b, body):
+        zero = jnp.zeros((step_rows, breadth), single)
+
+        def step(n, sums):
+            return body(n // steps, n % steps, sums)
+
+        sums = lax.fori_loop(0, depth * steps, step, (zero,) * (4 * bands))
+        at = pl.ds(pl.multiple_of(b * 4 * bands, 4 * bands), 4 * bands)
+        sums_ref[me, at, :] = jnp.concatenate(
+            [jnp.sum(v, axis=0, keepdims=True) for v in sums], axis=0
+        )
+
+    def home_result(row, i, sums):
+        waves = Waves(me, row, i)
+        pairs = []
+        for p in range(2):
+            theta = theta_at(waves, p, row, i)
+            for c in range(3):
+                theta_ref[p, c, side, row, rows_of(i), :] = theta[c]
+            pairs.append(waves.reduce(theta))
+        return add_sums(waves, pairs, row, i, sums)
+
+    def away_result(row, i, sums):
+        waves = Waves(me, row, i)
+        ratios = waves.ratios()
+        pairs = []
+        for p in range(2):
+            pair = [return_ref[row, n, p, rows_of(i), :] for n in range(2)]
+            theta = waves.rebuild(ratios, *pair)
+            for c in range(3):
+                theta_ref[p, c, 1 - side, row, rows_of(i), :] = theta[c]
+            pairs.append(pair)
+        return add_sums(waves, pairs, row, i, sums)
 
     def sums_copy(slot, peer, k):
         return pltpu.make_async_remote_copy(
@@ -507,68 +756,35 @@
             device_id_type=MESH,
         )
 
-    def make_sums():
-        def add(z, sums):
-            sums = list(sums)
-            for c in range(3):
-                ours = [(scaled_ref[b, c, 0, z], scaled_ref[b, c, 1, z]) for b in range(bands)]
-                fields = [
-                    (source[a, c, 0, z], source[a, c, 1, z])
-                    for source in (field_ref, other_ref)
-                    for a in range(bands)
-                ]
-                n = 0
-                for t_real, t_imag in ours:
-                    for real, imag in fields:
-                        sums[n] = sums[n] + (real * t_real + imag * t_imag)
-                        sums[n + 1] = sums[n + 1] + (real * t_imag - imag * t_real)
-                        n += 2
-            return tuple(sums)
-
-        zero = jnp.zeros((columns, breadth), single)
-        sums = lax.fori_loop(0, total, add, (zero,) * (4 * bands * bands))
-        sums_ref[me] = jnp.concatenate([jnp.sum(v, axis=0, keepdims=True) for v in sums], axis=0)
+    take_planes(1)
+    each_step(guest_result)
+    for row in range(depth):
+        return_copy(row).start()
+    take_planes(0)
+    other_copy(1 - side, 0).wait_recv()
+    other_copy(side, 1).wait_recv()
+    each_sum(side, home_result)
 
     half_copy(mine).wait_send()
     each_peer(lambda k, peer, source: slab_copy(peer, me, k).wait_send())
-    for b in range(bands):
-        drain_all(out1_ref, in1_ref, send1, recv1, b)
-
-    for b in range(bands):
-        if b == bands - 1:
-            for a in range(bands):
-                other_copy(a).wait_send()
-                other_copy(a).wait_recv()
-            make_sums()
-            each_peer(lambda k, peer, source: sums_copy(me, peer, k).start())
-            for a in range(b):
-                drain_all(out2_ref, in2_ref, send2, recv2, a)
-        finish_all(out2_ref, in2_ref, send2, recv2, b)
-
-        def plane_of(c, carry):
-            planes = jnp.concatenate(
-                [
-                    jnp.concatenate(
-                        [in2_ref[b, :, c, p, z].reshape(height, breadth) for p in range(2)], axis=1
-                    )
-                    for z in range(depth)
-                ],
-                axis=0,
-            )
-            wide = product(halves(planes), turned_table())
-            back_ref[c] = product(plain_table(), halves(spread_blocks(wide)))
-            return carry
-
-        lax.fori_loop(0, 3, plane_of, 0)
-
-        for z in range(depth):
-            for p in range(2):
-                rows, lanes = pl.ds(p * height, height), pl.ds(z * breadth, breadth)
-                crossed = cross([back_ref[c, rows, lanes] for c in range(3)], z)
-                for c in range(3):
-                    theta_ref[p, c, b, z] = -crossed[c]
-
-    drain_all(out2_ref, in2_ref, send2, recv2, bands - 1)
+    for row in range(depth):
+        swap_copy(row).wait_send()
+    other_copy(1 - side, 0).wait_send()
+    other_copy(side, 1).wait_send()
+
+    def drain(c, carry):
+        for s in range(2):
+            drain_all(*first, s, c, ends1(s))
+            drain_all(*second, s, c, ends2(s))
+        return carry
+
+    lax.fori_loop(0, 3, drain, 0)
+    for row in range(depth):
+        return_copy(row).wait_recv()
+    each_sum(1 - side, away_result)
+    each_peer(lambda k, peer, source: sums_copy(me, peer, k).start())
+    for row in range(depth):
+        return_copy(row).wait_send()
     each_peer(lambda k, peer, source: sums_copy(source, source, k).wait_recv())
     gram_ref[...] = jnp.sum(sums_ref[...], axis=0)
     each_peer(lambda k, peer, source: sums_copy(me, peer, k).wait_send())
@@ -578,14 +794,20 @@
     groups = lax.axis_size("gz")
     _, comps, bands, depth, height, breadth = coeffs.shape
     total = depth * groups
-    columns = height // groups
+    members = groups // 2
+    columns = height // members
     table = jnp.asarray(split_table(breadth, total**-0.25))
     grams = bands * 4 * bands
-    voxels = (bands, 3, 2, total, columns, breadth)
-    block = (bands, groups, 3, 2, depth, columns, breadth)
+    voxels = (3, 2, total, columns, breadth)
+    block = (2, members, 3, 2, depth, columns, breadth)
+    pairs = (depth, 2, 2, height, breadth)
     vmem = pl.BlockSpec(memory_space=pltpu.VMEM)
     hbm = pl.BlockSpec(memory_space=pltpu.HBM)
     dma = pltpu.SemaphoreType.DMA
+    operands = [
+        pltpu.with_memory_space_constraint(v, pltpu.HBM)
+        for v in (coeffs, material, inv_diag, inv_off, table)
+    ]
     theta, sums = pl.pallas_call(
         functools.partial(operator_kernel, groups),
         out_shape=(
@@ -605,24 +827,32 @@
             pltpu.VMEM((3, 2 * height, depth * breadth), half),
             pltpu.VMEM((3, 2 * height, depth * breadth), half),
             pltpu.VMEM((3, 2 * height, depth * breadth), single),
-            pltpu.VMEM(voxels, single),
+            pltpu.VMEM((bands, *pairs), single),
+            pltpu.VMEM((bands, *pairs), single),
+            pltpu.VMEM(pairs, single),
+            pltpu.VMEM(pairs, single),
+            pltpu.VMEM(pairs, single),
+            pltpu.VMEM(block, single),
+            pltpu.VMEM(block, single),
             pltpu.VMEM(voxels, single),
             pltpu.VMEM(voxels, single),
             pltpu.VMEM(block, single),
             pltpu.VMEM(block, single),
-            pltpu.VMEM(block, single),
-            pltpu.VMEM(block, single),
             pltpu.VMEM((groups, grams, breadth), single),
-            dma((5,)),
+            dma((6,)),
             dma((groups,)),
             dma((groups,)),
             dma((2,)),
-            dma((bands, groups)),
-            dma((bands, groups)),
-            dma((bands, groups)),
-            dma((bands, groups)),
-            dma((bands,)),
-            dma((bands,)),
+            dma((2, 3, members)),
+            dma((2, 3, members)),
+            dma((2, 3, members)),
+            dma((2, 3, members)),
+            dma((depth,)),
+            dma((depth,)),
+            dma((depth,)),
+            dma((depth,)),
+            dma((2,)),
+            dma((2,)),
             dma((groups,)),
             dma((groups,)),
         ],
@@ -630,7 +860,7 @@
             collective_id=0, has_side_effects=True, vmem_limit_bytes=48 * 1024 * 1024
         ),
         name="maxwell",
-    )(coeffs, material, inv_diag, inv_off, table)
+    )(*operands)
     values = jnp.sum(sums, axis=1) / (breadth * height * total)
     values = values.reshape(bands, 2, bands, 2).transpose(1, 3, 2, 0)
     own, other = values[0], values[1]
@@ -640,16 +870,15 @@
 
 
 def fits(coeffs):
-    groups, depth, height, breadth = (
-        lax.axis_size("gz"),
-        coeffs.shape[3],
-        coeffs.shape[4],
-        coeffs.shape[5],
-    )
+    groups = lax.axis_size("gz")
+    _, _, bands, depth, height, breadth = coeffs.shape
     return (
         lax.axis_size("ba") == 2
+        and bands == 2
         and depth == 2
-        and height % (8 * groups) == 0
+        and groups >= 4
+        and height % (4 * groups) == 0
+        and height % 16 == 0
         and height == breadth
         and breadth % 128 == 0
     )

time: 89.9 us -> 90.7 us (level)
  Pallas kernels: 82 us -> 87.7 us
  local copies, waits for them, and re-layouts: 6.82 us -> 2.11 us
    pallas_call x1, Pallas kernels: 82 us -> 87.7 us  [on_device_kernel(): pl.pallas_call(functools.partial(operator_kernel, groups), out_shape=(jax...]
    unnamed x12 -> x2, local copies, waits for them, and re-layouts: 6.53 us -> 1.82 us
where the time goes in v3:
time: 90.7 us; the launch traced here: 90.6 us
  Pallas kernels  87.7 us (97%)
  local copies, waits for them, and re-layouts  2.11 us (2%)
    pallas_call x1, Pallas kernels, on_device_kernel(): pl.pallas_call(functools.partial(operator_kernel, groups), out_shape=(jax...  87.7 us
    unnamed x2, local copies, waits for them, and re-layouts  1.82 us

profile of v3, /device:TPU:0, one launch (start us, length us, event | category | flops | bytes accessed | tf_op | source)
XLA Modules:
  0.0 90.6 jit_solution(17251233919787985225)
XLA Ops:
  0.6 87.7 %maxwell.1 = (f32[2,3,2,2,128,128]{5,4,3,2,1,0:T(8,128)S(1)}, f32[16,128]{1,0:T(8,128)S(1)}) custom-call(f32[2,3,2,2,128,128]{5,4,3,2,1,0:T(8,128)} %coeffs_hbm.1, s32[2,128,128]{2,1,0:T(8,128)} %material_hbm.1, f32[4,3]{1,0:T(4,128)} %diag_hbm.1, f32[4,3]{1,0:T(4,128)} %off_hbm.1, bf16[4,256,256]{2,1,0:T(8,128)(2,1)} %constant.13.clone.table_hbm), custom_call_target="tpu_custom_call" | custom-call | tf_op jit(solution)/shard_map/maxwell/pallas_call | solution.py:811
  88.3 0.1 reduce_sum.9
  88.4 0.1 div.6
  88.5 0.1 copy.7
  88.6 0.1 copy.8
  88.7 0.7 copy.9
  89.4 1.1 %copy.11 = f32[2,3,2,2,128,128]{5,4,3,2,1,0:T(8,128)} copy(f32[2,3,2,2,128,128]{5,4,3,2,1,0:T(8,128)S(1)} %get-tuple-element.12) | data formatting | bytes 3145728
  (3 shorter events, 0.0 us)

commit v4 on v3

--- a/solution.py
+++ b/solution.py
@@ -373,20 +373,27 @@
     def rows_of(i):
         return pl.ds(pl.multiple_of(i * step_rows, step_rows), step_rows)
 
-    def each_step(body):
-        def step(n, carry):
-            body(n // steps, n % steps)
+    def each_step(row, body):
+        def step(i, carry):
+            body(row, i)
             return carry
 
-        lax.fori_loop(0, depth * steps, step, 0)
+        lax.fori_loop(0, steps, step, 0)
+
+    def each_row(body):
+        def step(row, carry):
+            body(row)
+            return carry
+
+        lax.fori_loop(0, depth, step, 0)
 
     def put_halves(curls, p, row, i):
         at = pl.ds(pl.multiple_of(p * height + i * step_rows, step_rows), step_rows)
-        lanes = pl.ds(pl.multiple_of(row * breadth, breadth), breadth)
         for c in range(3):
             high, low = halves(curls[c])
-            high_ref[c, at, lanes] = high
-            low_ref[c, at, lanes] = low
+            lanes = pl.ds(c * breadth, breadth)
+            high_ref[row, at, lanes] = high
+            low_ref[row, at, lanes] = low
 
     def put_pair(b, p, row, i, pair):
         for n in range(2):
@@ -430,7 +437,7 @@
                     ],
                     axis=1,
                 )
-                for z in range(depth)
+                for z in range(3)
             ],
             axis=0,
         )
@@ -441,7 +448,7 @@
                 jnp.concatenate(
                     [
                         values[z * height : (z + 1) * height, p * breadth : (p + 1) * breadth]
-                        for z in range(depth)
+                        for z in range(3)
                     ],
                     axis=1,
                 )
@@ -450,22 +457,22 @@
             axis=0,
         )
 
-    def to_peer(out, into, send, recv, s, c, k, peer, from_at, to_at):
+    def to_peer(out, into, send, recv, s, row, k, peer, from_at, to_at):
         return pltpu.make_async_remote_copy(
-            src_ref=out.at[from_at, peer, c],
-            dst_ref=into.at[to_at, seat, c],
-            send_sem=send.at[s, c, k],
-            recv_sem=recv.at[s, c, k],
+            src_ref=out.at[from_at, row, peer],
+            dst_ref=into.at[to_at, row, seat],
+            send_sem=send.at[s, row, k],
+            recv_sem=recv.at[s, row, k],
             device_id={"gz": side * members + peer},
             device_id_type=MESH,
         )
 
-    def from_peer(out, into, send, recv, s, c, k, source, from_at, to_at):
+    def from_peer(out, into, send, recv, s, row, k, source, from_at, to_at):
         return pltpu.make_async_remote_copy(
-            src_ref=out.at[from_at, source, c],
-            dst_ref=into.at[to_at, source, c],
-            send_sem=send.at[s, c, k],
-            recv_sem=recv.at[s, c, k],
+            src_ref=out.at[from_at, row, source],
+            dst_ref=into.at[to_at, row, source],
+            send_sem=send.at[s, row, k],
+            recv_sem=recv.at[s, row, k],
             device_id={"gz": side * members + source},
             device_id_type=MESH,
         )
@@ -476,43 +483,39 @@
     def ends2(s):
         return (side + s) % 2, s
 
-    def start_all(out, into, send, recv, s, c, ends):
+    def start_all(out, into, send, recv, s, row, ends):
         each_member(
             lambda k, peer, source: to_peer(
-                out, into, send, recv, s, c, k, peer, *ends
+                out, into, send, recv, s, row, k, peer, *ends
             ).start()
         )
-        into[ends[1], seat, c] = out[ends[0], seat, c]
-
-    def finish_all(out, into, send, recv, s, c, ends):
+        into[ends[1], row, seat] = out[ends[0], row, seat]
+
+    def finish_all(out, into, send, recv, s, row, ends):
         each_member(
             lambda k, peer, source: from_peer(
-                out, into, send, recv, s, c, k, source, *ends
+                out, into, send, recv, s, row, k, source, *ends
             ).wait_recv()
         )
 
-    def drain_all(out, into, send, recv, s, c, ends):
+    def drain_all(out, into, send, recv, s, row, ends):
         each_member(
             lambda k, peer, source: to_peer(
-                out, into, send, recv, s, c, k, peer, *ends
+                out, into, send, recv, s, row, k, peer, *ends
             ).wait_send()
         )
 
     first = (out1_ref, in1_ref, send1, recv1)
     second = (out2_ref, in2_ref, send2, recv2)
 
-    def make_planes(s):
-        def one(c, carry):
-            tall = product(turned_table(), (high_ref[c], low_ref[c]))
-            wide = product(halves(gather_blocks(tall)), plain_table())
-            for p in range(2):
-                for z in range(depth):
-                    plane = wide[z * height : (z + 1) * height, p * breadth : (p + 1) * breadth]
-                    out1_ref[s, :, c, p, z] = plane.reshape(members, columns, breadth)
-            start_all(*first, s, c, ends1(s))
-            return carry
-
-        lax.fori_loop(0, 3, one, 0)
+    def make_planes(s, row):
+        tall = product(turned_table(), (high_ref[row], low_ref[row]))
+        wide = product(halves(gather_blocks(tall)), plain_table())
+        for p in range(2):
+            for c in range(3):
+                plane = wide[c * height : (c + 1) * height, p * breadth : (p + 1) * breadth]
+                out1_ref[s, row, :, c, p] = plane.reshape(members, columns, breadth)
+        start_all(*first, s, row, ends1(s))
 
     def swap_copy(row):
         return pltpu.make_async_remote_copy(
@@ -557,40 +560,73 @@
             device_id_type=MESH,
         )
 
-    def half_copy(row):
+    def half_copy(row, part):
+        at = pl.ds(pl.multiple_of(part * members, members), members)
         return pltpu.make_async_remote_copy(
-            src_ref=slab_ref.at[row],
-            dst_ref=slab_ref.at[row],
-            send_sem=half_sem.at[0],
-            recv_sem=half_sem.at[1],
+            src_ref=slab_ref.at[row, at],
+            dst_ref=slab_ref.at[row, at],
+            send_sem=half_sem.at[0, part],
+            recv_sem=half_sem.at[1, part],
             device_id=mate,
             device_id_type=MESH,
         )
 
+    outer = (me // (members // 2)) % 3 == 0
+
     loads[0].wait()
-    each_step(away_step)
+    each_row(lambda row: each_step(row, away_step))
     pl.semaphore_wait(barrier, groups)
     swap_copy(0).start()
-    other_copy(1 - side, 0).start()
+
+    @pl.when(jnp.logical_not(outer))
+    def _():
+        swap_copy(1).start()
+
     loads[1].wait()
-    each_step(home_step)
+    loads[2].wait()
+
+    def home_row(row):
+        each_step(row, home_step)
+        make_planes(0, row)
+
+    each_row(home_row)
+
+    @pl.when(outer)
+    def _():
+        swap_copy(1).start()
+
     other_copy(side, 1).start()
-    loads[2].wait()
-    make_planes(0)
-    swap_copy(1).start()
     for load in loads[3:]:
         load.wait()
     each_peer(lambda k, peer, source: slab_copy(peer, me, k).start())
     slab_ref[mine, me] = material_ref[mine, columns_of(me), :]
 
-    for row in range(depth):
+    def wait_slabs(part):
+        def step(k, carry):
+            source = (me + groups - k) % groups
+
+            @pl.when(source // members == part)
+            def _():
+                slab_copy(source, source, k).wait_recv()
+
+            return carry
+
+        lax.fori_loop(1, groups, step, 0)
+
+    def guest_row(row):
         swap_copy(row).wait_recv()
-    each_step(guest_step)
-    make_planes(1)
-
-    each_peer(lambda k, peer, source: slab_copy(source, source, k).wait_recv())
-    half_copy(mine).start()
-    half_copy(1 - mine).wait_recv()
+        each_step(row, guest_step)
+        make_planes(1, row)
+
+    guest_row(0)
+    wait_slabs(side)
+    half_copy(mine, side).start()
+    guest_row(1)
+    wait_slabs(1 - side)
+    half_copy(mine, 1 - side).start()
+    other_copy(1 - side, 0).start()
+    for part in range(2):
+        half_copy(1 - mine, part).wait_recv()
     kinds = diag_ref.shape[0]
 
     def tensor_step(owner, carry):
@@ -609,26 +645,25 @@
     def part_of(n):
         return pl.ds(pl.multiple_of(n * 8, 8), 8)
 
-    def inverse(c, carry):
+    def finish_first(row):
         for s in range(2):
-            finish_all(*first, s, c, ends1(s))
-
-        def part(n, carry):
-            points = []
-            for r in range(total):
-                owner, row = r // depth, r % depth
-                at = (owner // members, owner % members, c)
-                points.append(
-                    (in1_ref[(*at, 0, row, part_of(n))], in1_ref[(*at, 1, row, part_of(n))])
-                )
-            for z, (real, imag) in enumerate(to_voxels(points)):
-                field_ref[c, 0, z, part_of(n)] = real
-                field_ref[c, 1, z, part_of(n)] = imag
-            return carry
-
-        return lax.fori_loop(0, columns // 8, part, carry)
-
-    lax.fori_loop(0, 3, inverse, 0)
+            finish_all(*first, s, row, ends1(s))
+
+    each_row(finish_first)
+
+    def inverse(n, carry):
+        c, at = n // (columns // 8), part_of(n % (columns // 8))
+        points = []
+        for r in range(total):
+            owner, row = r // depth, r % depth
+            where = (owner // members, row, owner % members, c)
+            points.append((in1_ref[(*where, 0, at)], in1_ref[(*where, 1, at)]))
+        for z, (real, imag) in enumerate(to_voxels(points)):
+            field_ref[c, 0, z, at] = real
+            field_ref[c, 1, z, at] = imag
+        return carry
+
+    lax.fori_loop(0, 3 * (columns // 8), inverse, 0)
 
     def scale(z, carry):
         xx, yy, zz, xy, yz, zx = [tensor_ref[entry, z // depth, z % depth] for entry in range(6)]
@@ -641,53 +676,38 @@
 
     lax.fori_loop(0, total, scale, 0, unroll=2)
 
-    def forward(c, carry):
-        def part(n, carry):
-            points = [
-                (scaled_ref[c, 0, z, part_of(n)], scaled_ref[c, 1, z, part_of(n)])
-                for z in range(total)
-            ]
-            for r, (real, imag) in enumerate(to_waves(points)):
-                owner, row = r // depth, r % depth
-                at = (owner // members, owner % members, c)
-                out2_ref[(*at, 0, row, part_of(n))] = real
-                out2_ref[(*at, 1, row, part_of(n))] = imag
-            return carry
-
-        lax.fori_loop(0, columns // 8, part, 0)
-        start_all(*second, 1, c, ends2(1))
+    def forward(n, carry):
+        c, at = n // (columns // 8), part_of(n % (columns // 8))
+        points = [(scaled_ref[c, 0, z, at], scaled_ref[c, 1, z, at]) for z in range(total)]
+        for r, (real, imag) in enumerate(to_waves(points)):
+            owner, row = r // depth, r % depth
+            where = (owner // members, row, owner % members, c)
+            out2_ref[(*where, 0, at)] = real
+            out2_ref[(*where, 1, at)] = imag
         return carry
 
-    lax.fori_loop(0, 3, forward, 0)
-
-    def start_home(c, carry):
-        start_all(*second, 0, c, ends2(0))
-        return carry
-
-    lax.fori_loop(0, 3, start_home, 0)
-
-    def take_planes(s):
-        def one(c, carry):
-            finish_all(*second, s, c, ends2(s))
-            planes = jnp.concatenate(
-                [
-                    jnp.concatenate(
-                        [in2_ref[s, :, c, p, z].reshape(height, breadth) for p in range(2)], axis=1
-                    )
-                    for z in range(depth)
-                ],
-                axis=0,
-            )
-            wide = product(halves(planes), turned_table())
-            back_ref[c] = product(plain_table(), halves(spread_blocks(wide)))
-            return carry
-
-        lax.fori_loop(0, 3, one, 0)
+    lax.fori_loop(0, 3 * (columns // 8), forward, 0)
+    each_row(lambda row: start_all(*second, 1, row, ends2(1)))
+    each_row(lambda row: start_all(*second, 0, row, ends2(0)))
+
+    def take_planes(s, row):
+        finish_all(*second, s, row, ends2(s))
+        planes = jnp.concatenate(
+            [
+                jnp.concatenate(
+                    [in2_ref[s, row, :, c, p].reshape(height, breadth) for p in range(2)], axis=1
+                )
+                for c in range(3)
+            ],
+            axis=0,
+        )
+        wide = product(halves(planes), turned_table())
+        back_ref[row] = product(plain_table(), halves(spread_blocks(wide)))
 
     def theta_at(waves, p, row, i):
         at = pl.ds(pl.multiple_of(p * height + i * step_rows, step_rows), step_rows)
-        lanes = pl.ds(pl.multiple_of(row * breadth, breadth), breadth)
-        return [-v for v in waves.cross([back_ref[c, at, lanes] for c in range(3)])]
+        lanes = [pl.ds(c * breadth, breadth) for c in range(3)]
+        return [-v for v in waves.cross([back_ref[row, at, lanes[c]] for c in range(3)])]
 
     def guest_result(row, i):
         waves = Waves(partner, row, i)
@@ -712,13 +732,13 @@
                 n += 2
         return tuple(sums)
 
-    def each_sum(b, body):
-        zero = jnp.zeros((step_rows, breadth), single)
-
-        def step(n, sums):
-            return body(n // steps, n % steps, sums)
-
-        sums = lax.fori_loop(0, depth * steps, step, (zero,) * (4 * bands))
+    def zero_sums():
+        return (jnp.zeros((step_rows, breadth), single),) * (4 * bands)
+
+    def each_sum(row, body, sums):
+        return lax.fori_loop(0, steps, lambda i, sums: body(row, i, sums), sums)
+
+    def keep_sums(b, sums):
         at = pl.ds(pl.multiple_of(b * 4 * bands, 4 * bands), 4 * bands)
         sums_ref[me, at, :] = jnp.concatenate(
             [jnp.sum(v, axis=0, keepdims=True) for v in sums], axis=0
@@ -756,32 +776,41 @@
             device_id_type=MESH,
         )
 
-    take_planes(1)
-    each_step(guest_result)
-    for row in range(depth):
+    def guest_back(row):
+        take_planes(1, row)
+        each_step(row, guest_result)
         return_copy(row).start()
-    take_planes(0)
+
+    each_row(guest_back)
+
+    def home_back(row, sums):
+        take_planes(0, row)
+        return each_sum(row, home_result, sums)
+
+    other_copy(side, 1).wait_recv()
     other_copy(1 - side, 0).wait_recv()
-    other_copy(side, 1).wait_recv()
-    each_sum(side, home_result)
-
-    half_copy(mine).wait_send()
+    keep_sums(side, lax.fori_loop(0, depth, home_back, zero_sums()))
+
+    for part in range(2):
+        half_copy(mine, part).wait_send()
     each_peer(lambda k, peer, source: slab_copy(peer, me, k).wait_send())
     for row in range(depth):
         swap_copy(row).wait_send()
     other_copy(1 - side, 0).wait_send()
     other_copy(side, 1).wait_send()
 
-    def drain(c, carry):
+    def drain(row):
         for s in range(2):
-            drain_all(*first, s, c, ends1(s))
-            drain_all(*second, s, c, ends2(s))
-        return carry
-
-    lax.fori_loop(0, 3, drain, 0)
-    for row in range(depth):
+            drain_all(*first, s, row, ends1(s))
+            drain_all(*second, s, row, ends2(s))
+
+    each_row(drain)
+
+    def away_back(row, sums):
         return_copy(row).wait_recv()
-    each_sum(1 - side, away_result)
+        return each_sum(row, away_result, sums)
+
+    keep_sums(1 - side, lax.fori_loop(0, depth, away_back, zero_sums()))
     each_peer(lambda k, peer, source: sums_copy(me, peer, k).start())
     for row in range(depth):
         return_copy(row).wait_send()
@@ -799,7 +828,7 @@
     table = jnp.asarray(split_table(breadth, total**-0.25))
     grams = bands * 4 * bands
     voxels = (3, 2, total, columns, breadth)
-    block = (2, members, 3, 2, depth, columns, breadth)
+    block = (2, depth, members, 3, 2, columns, breadth)
     pairs = (depth, 2, 2, height, breadth)
     vmem = pl.BlockSpec(memory_space=pltpu.VMEM)
     hbm = pl.BlockSpec(memory_space=pltpu.HBM)
@@ -824,9 +853,9 @@
             pltpu.SMEM(inv_off.shape, single),
             pltpu.VMEM((depth, groups, columns, breadth), jnp.int32),
             pltpu.VMEM((6, groups, depth, columns, breadth), single),
-            pltpu.VMEM((3, 2 * height, depth * breadth), half),
-            pltpu.VMEM((3, 2 * height, depth * breadth), half),
-            pltpu.VMEM((3, 2 * height, depth * breadth), single),
+            pltpu.VMEM((depth, 2 * height, 3 * breadth), half),
+            pltpu.VMEM((depth, 2 * height, 3 * breadth), half),
+            pltpu.VMEM((depth, 2 * height, 3 * breadth), single),
             pltpu.VMEM((bands, *pairs), single),
             pltpu.VMEM((bands, *pairs), single),
             pltpu.VMEM(pairs, single),
@@ -842,11 +871,11 @@
             dma((6,)),
             dma((groups,)),
             dma((groups,)),
-            dma((2,)),
-            dma((2, 3, members)),
-            dma((2, 3, members)),
-            dma((2, 3, members)),
-            dma((2, 3, members)),
+            dma((2, 2)),
+            dma((2, depth, members)),
+            dma((2, depth, members)),
+            dma((2, depth, members)),
+            dma((2, depth, members)),
             dma((depth,)),
             dma((depth,)),
             dma((depth,)),

time: 90.7 us -> 81.9 us (0.903)
  Pallas kernels: 87.7 us -> 78.8 us
    pallas_call x1, Pallas kernels: 87.7 us -> 78.8 us  [on_device_kernel(): pl.pallas_call(functools.partial(operator_kernel, groups), out_shape=(jax...]
where the time goes in v4:
time: 81.9 us; the launch traced here: 81.7 us
  Pallas kernels  78.8 us (96%)
  local copies, waits for them, and re-layouts  2.11 us (3%)
    pallas_call x1, Pallas kernels, on_device_kernel(): pl.pallas_call(functools.partial(operator_kernel, groups), out_shape=(jax...  78.8 us
    unnamed x2, local copies, waits for them, and re-layouts  1.82 us

profile of v4, /device:TPU:0, one launch (start us, length us, event | category | flops | bytes accessed | tf_op | source)
XLA Modules:
  0.0 81.7 jit_solution(4388821323634498957)
XLA Ops:
  0.6 78.8 %maxwell.1 = (f32[2,3,2,2,128,128]{5,4,3,2,1,0:T(8,128)S(1)}, f32[16,128]{1,0:T(8,128)S(1)}) custom-call(f32[2,3,2,2,128,128]{5,4,3,2,1,0:T(8,128)} %coeffs_hbm.1, s32[2,128,128]{2,1,0:T(8,128)} %material_hbm.1, f32[4,3]{1,0:T(4,128)} %diag_hbm.1, f32[4,3]{1,0:T(4,128)} %off_hbm.1, bf16[4,256,256]{2,1,0:T(8,128)(2,1)} %constant.13.clone.table_hbm), custom_call_target="tpu_custom_call" | custom-call | tf_op jit(solution)/shard_map/maxwell/pallas_call | solution.py:840
  79.5 0.1 reduce_sum.9
  79.6 0.1 div.6
  79.7 0.1 copy.7
  79.8 0.1 copy.8
  79.9 0.7 copy.9
  80.6 1.1 %copy.11 = f32[2,3,2,2,128,128]{5,4,3,2,1,0:T(8,128)} copy(f32[2,3,2,2,128,128]{5,4,3,2,1,0:T(8,128)S(1)} %get-tuple-element.12) | data formatting | bytes 3145728
  (3 shorter events, 0.0 us)

commit v5 on v4

--- a/solution.py
+++ b/solution.py
@@ -237,6 +237,9 @@
     scaled_ref,
     out2_ref,
     in2_ref,
+    out3_ref,
+    in3_ref,
+    acc_ref,
     sums_ref,
     load_sem,
     slab_send,
@@ -246,6 +249,10 @@
     recv1,
     send2,
     recv2,
+    send3,
+    recv3,
+    send4,
+    recv4,
     swap_send,
     swap_recv,
     return_send,
@@ -265,6 +272,12 @@
     side = me // members
     seat = me % members
     partner = (me + members) % groups
+    pack = members // 2
+    inner = seat // pack == 1 - side
+    outer = jnp.logical_not(inner)
+    odd = seat % 2 == 1
+    direct = jnp.logical_and(inner, jnp.logical_not(odd))
+    second_guest = jnp.logical_or(inner, odd)
     mate = {"ba": 1 - mine}
     step_rows = 16
     steps = height // step_rows
@@ -291,19 +304,21 @@
     )
     pl.semaphore_signal(barrier, inc=1, device_id=mate, device_id_type=MESH)
 
-    def band_load(b, n):
+    def row_load(b, row, n):
         return pltpu.make_async_copy(
-            coeffs_hbm.at[:, :, b], coeffs_ref.at[:, :, b], load_sem.at[n]
+            coeffs_hbm.at[:, :, b, row], coeffs_ref.at[:, :, b, row], load_sem.at[n, row]
         )
 
     loads = [
-        band_load(1 - side, 0),
-        band_load(side, 1),
-        pltpu.make_async_copy(table_hbm, table_ref, load_sem.at[2]),
-        pltpu.make_async_copy(material_hbm, material_ref, load_sem.at[3]),
-        pltpu.make_async_copy(diag_hbm, diag_ref, load_sem.at[4]),
-        pltpu.make_async_copy(off_hbm, off_ref, load_sem.at[5]),
+        pltpu.make_async_copy(table_hbm, table_ref, load_sem.at[2, 0]),
+        pltpu.make_async_copy(material_hbm, material_ref, load_sem.at[2, 1]),
+        pltpu.make_async_copy(diag_hbm, diag_ref, load_sem.at[3, 0]),
+        pltpu.make_async_copy(off_hbm, off_ref, load_sem.at[3, 1]),
     ]
+    for row in range(depth):
+        row_load(1 - side, row, 0).start()
+    for row in range(depth):
+        row_load(side, row, 1).start()
     for load in loads:
         load.start()
 
@@ -413,6 +428,12 @@
             put_halves(curls, p, row, i)
             put_pair(side, p, row, i, waves.reduce(curls))
 
+    def direct_step(row, i):
+        waves = Waves(me, row, i)
+        for p in range(2):
+            values = [coeffs_ref[p, c, 1 - side, row, rows_of(i), :] for c in range(3)]
+            put_halves(waves.cross(values), p, row, i)
+
     def guest_step(row, i):
         waves = Waves(partner, row, i)
         ratios = waves.ratios()
@@ -491,6 +512,74 @@
         )
         into[ends[1], row, seat] = out[ends[0], row, seat]
 
+    def is_inner(peer):
+        return peer // pack == 1 - side
+
+    def each_inner(body):
+        def one(k, peer, source):
+            pl.when(is_inner(peer))(lambda: body(k, peer))
+
+        each_member(one)
+
+    def each_second_source(body):
+        def one(k, peer, source):
+            has_guest = jnp.logical_or(is_inner(source), source % 2 == 1)
+            pl.when(has_guest)(lambda: body(k, source))
+
+        each_member(one)
+
+    def across(peer):
+        return {"gz": (1 - side) * members + peer}
+
+    def direct_copy(peer):
+        return pltpu.make_async_remote_copy(
+            src_ref=out3_ref.at[peer],
+            dst_ref=in1_ref.at[side, 1, seat],
+            send_sem=send3.at[peer],
+            recv_sem=recv3.at[seat % pack // 2],
+            device_id=across(peer),
+            device_id_type=MESH,
+        )
+
+    def direct_arrival(n):
+        source = side * pack + 2 * n
+        return pltpu.make_async_remote_copy(
+            src_ref=out3_ref.at[source],
+            dst_ref=in1_ref.at[1 - side, 1, source],
+            send_sem=send3.at[source],
+            recv_sem=recv3.at[n],
+            device_id=across(source),
+            device_id_type=MESH,
+        )
+
+    def direct_result(n):
+        peer = side * pack + n
+        return pltpu.make_async_remote_copy(
+            src_ref=out2_ref.at[1 - side, 1, peer],
+            dst_ref=in3_ref.at[seat],
+            send_sem=send4.at[n],
+            recv_sem=recv4.at[seat],
+            device_id=across(peer),
+            device_id_type=MESH,
+        )
+
+    def result_arrival(source):
+        return pltpu.make_async_remote_copy(
+            src_ref=out2_ref.at[1 - side, 1, source],
+            dst_ref=in3_ref.at[source],
+            send_sem=send4.at[source % pack],
+            recv_sem=recv4.at[source],
+            device_id=across(source),
+            device_id_type=MESH,
+        )
+
+    def each_of(count, body):
+        def step(n, carry):
+            body(n)
+            return carry
+
+        lax.fori_loop(0, count, step, 0)
+
     def finish_all(out, into, send, recv, s, row, ends):
         each_member(
             lambda k, peer, source: from_peer(
@@ -508,14 +597,19 @@
     first = (out1_ref, in1_ref, send1, recv1)
     second = (out2_ref, in2_ref, send2, recv2)
 
-    def make_planes(s, row):
+    def planes_into(put, row):
         tall = product(turned_table(), (high_ref[row], low_ref[row]))
         wide = product(halves(gather_blocks(tall)), plain_table())
         for p in range(2):
             for c in range(3):
                 plane = wide[c * height : (c + 1) * height, p * breadth : (p + 1) * breadth]
-                out1_ref[s, row, :, c, p] = plane.reshape(members, columns, breadth)
-        start_all(*first, s, row, ends1(s))
+                put(c, p, plane.reshape(members, columns, breadth))
+
+    def make_planes(s, row):
+        def put(c, p, block):
+            out1_ref[s, row, :, c, p] = block
+
+        planes_into(put, row)
 
     def swap_copy(row):
         return pltpu.make_async_remote_copy(
@@ -571,62 +665,76 @@
             device_id_type=MESH,
         )
 
-    outer = (me // (members // 2)) % 3 == 0
-
-    loads[0].wait()
-    each_row(lambda row: each_step(row, away_step))
+    def away_row(row):
+        row_load(1 - side, row, 0).wait()
+        each_step(row, away_step)
+
+    def home_row(row):
+        row_load(side, row, 1).wait()
+        each_step(row, home_step)
+        make_planes(0, row)
+        start_all(*first, 0, row, ends1(0))
+
+    def start_slabs(base):
+        def step(k, carry):
+            peer = base * members + (seat + k) % members
+            slab_copy(peer, me, (peer + groups - me) % groups).start()
+            return carry
+
+        return step
+
+    def wait_slabs(base):
+        def step(k, carry):
+            source = base * members + (seat + members - k) % members
+            slab_copy(source, source, (me + groups - source) % groups).wait_recv()
+            return carry
+
+        return step
+
+    away_row(0)
     pl.semaphore_wait(barrier, groups)
     swap_copy(0).start()
-
-    @pl.when(jnp.logical_not(outer))
-    def _():
-        swap_copy(1).start()
-
-    loads[1].wait()
-    loads[2].wait()
-
-    def home_row(row):
-        each_step(row, home_step)
-        make_planes(0, row)
-
-    each_row(home_row)
-
-    @pl.when(outer)
-    def _():
-        swap_copy(1).start()
-
+    for load in loads:
+        load.wait()
+    lax.fori_loop(1, members, start_slabs(side), 0)
+    lax.fori_loop(0, members, start_slabs(1 - side), 0)
+    away_row(1)
+    pl.when(jnp.logical_not(direct))(lambda: swap_copy(1).start())
+    slab_ref[mine, me] = material_ref[mine, columns_of(me), :]
+    home_row(0)
+    home_row(1)
+
+    def make_direct():
+        each_step(1, direct_step)
+
+        def put(c, p, block):
+            out3_ref[:, c, p] = block
+
+        planes_into(put, 1)
+
+    def send_direct():
+        each_of(members, lambda n: direct_copy((seat + n) % members).start())
+
+    pl.when(direct)(make_direct)
     other_copy(side, 1).start()
-    for load in loads[3:]:
-        load.wait()
-    each_peer(lambda k, peer, source: slab_copy(peer, me, k).start())
-    slab_ref[mine, me] = material_ref[mine, columns_of(me), :]
-
-    def wait_slabs(part):
-        def step(k, carry):
-            source = (me + groups - k) % groups
-
-            @pl.when(source // members == part)
-            def _():
-                slab_copy(source, source, k).wait_recv()
-
-            return carry
-
-        lax.fori_loop(1, groups, step, 0)
+    acc_ref[...] = jnp.zeros(acc_ref.shape, single)
 
     def guest_row(row):
         swap_copy(row).wait_recv()
         each_step(row, guest_step)
         make_planes(1, row)
+        start_all(*first, 1, row, ends1(1))
 
     guest_row(0)
-    wait_slabs(side)
+    lax.fori_loop(1, members, wait_slabs(side), 0)
     half_copy(mine, side).start()
-    guest_row(1)
-    wait_slabs(1 - side)
+    pl.when(inner)(lambda: guest_row(1))
+    lax.fori_loop(0, members, wait_slabs(1 - side), 0)
     half_copy(mine, 1 - side).start()
-    other_copy(1 - side, 0).start()
-    for part in range(2):
-        half_copy(1 - mine, part).wait_recv()
+    pl.when(direct)(send_direct)
+    pl.when(jnp.logical_and(outer, odd))(lambda: guest_row(1))
+    half_copy(1 - mine, side).wait_recv()
+    half_copy(1 - mine, 1 - side).wait_recv()
     kinds = diag_ref.shape[0]
 
     def tensor_step(owner, carry):
@@ -645,11 +753,10 @@
     def part_of(n):
         return pl.ds(pl.multiple_of(n * 8, 8), 8)
 
-    def finish_first(row):
-        for s in range(2):
-            finish_all(*first, s, row, ends1(s))
-
-    each_row(finish_first)
+    each_row(lambda row: finish_all(*first, 0, row, ends1(0)))
+    finish_all(*first, 1, 0, ends1(1))
+    each_second_source(lambda k, source: from_peer(*first, 1, 1, k, source, *ends1(1)).wait_recv())
+    each_of(pack // 2, lambda n: direct_arrival(n).wait_recv())
 
     def inverse(n, carry):
         c, at = n // (columns // 8), part_of(n % (columns // 8))
@@ -687,15 +794,26 @@
         return carry
 
     lax.fori_loop(0, 3 * (columns // 8), forward, 0)
-    each_row(lambda row: start_all(*second, 1, row, ends2(1)))
-    each_row(lambda row: start_all(*second, 0, row, ends2(0)))
-
-    def take_planes(s, row):
-        finish_all(*second, s, row, ends2(s))
+    start_all(*second, 1, 0, ends2(1))
+    each_of(pack, lambda n: direct_result((seat + n) % pack).start())
+    each_inner(lambda k, peer: to_peer(*second, 1, 1, k, peer, *ends2(1)).start())
+
+    def keep_guest():
+        in2_ref[1, 1, seat] = out2_ref[1 - side, 1, seat]
+
+    pl.when(inner)(keep_guest)
+
+    def start_home():
+        each_row(lambda row: start_all(*second, 0, row, ends2(0)))
+
+    pl.when(inner)(start_home)
+    other_copy(1 - side, 0).start()
+
+    def planes_back(get, row):
         planes = jnp.concatenate(
             [
                 jnp.concatenate(
-                    [in2_ref[s, row, :, c, p].reshape(height, breadth) for p in range(2)], axis=1
+                    [get(c, p).reshape(height, breadth) for p in range(2)], axis=1
                 )
                 for c in range(3)
             ],
@@ -703,6 +821,10 @@
         )
         wide = product(halves(planes), turned_table())
         back_ref[row] = product(plain_table(), halves(spread_blocks(wide)))
+
+    def take_planes(s, row):
+        finish_all(*second, s, row, ends2(s))
+        planes_back(lambda c, p: in2_ref[s, row, :, c, p], row)
 
     def theta_at(waves, p, row, i):
         at = pl.ds(pl.multiple_of(p * height + i * step_rows, step_rows), step_rows)
@@ -732,27 +854,39 @@
                 n += 2
         return tuple(sums)
 
-    def zero_sums():
-        return (jnp.zeros((step_rows, breadth), single),) * (4 * bands)
-
-    def each_sum(row, body, sums):
-        return lax.fori_loop(0, steps, lambda i, sums: body(row, i, sums), sums)
-
-    def keep_sums(b, sums):
-        at = pl.ds(pl.multiple_of(b * 4 * bands, 4 * bands), 4 * bands)
-        sums_ref[me, at, :] = jnp.concatenate(
-            [jnp.sum(v, axis=0, keepdims=True) for v in sums], axis=0
-        )
-
-    def home_result(row, i, sums):
-        waves = Waves(me, row, i)
-        pairs = []
-        for p in range(2):
-            theta = theta_at(waves, p, row, i)
-            for c in range(3):
-                theta_ref[p, c, side, row, rows_of(i), :] = theta[c]
-            pairs.append(waves.reduce(theta))
-        return add_sums(waves, pairs, row, i, sums)
+    def each_sum(row, b, body):
+        def step(i, sums):
+            return body(row, i, sums)
+
+        sums = lax.fori_loop(0, steps, step, tuple(acc_ref[b, n] for n in range(4 * bands)))
+        for n in range(4 * bands):
+            acc_ref[b, n] = sums[n]
+
+    def keep_sums(b):
+        sums = [acc_ref[b, n] for n in range(4 * bands)]
+        lane = lax.broadcasted_iota(jnp.int32, (1, breadth), 1)
+        rows = [jnp.zeros((1, breadth), single)] * 2
+        n = 0
+        for source in (mine, 1 - mine):
+            for a in range(bands):
+                for p in range(2):
+                    value = jnp.sum(jnp.sum(sums[n], axis=0, keepdims=True), axis=1, keepdims=True)
+                    rows[p] = rows[p] + jnp.where(lane == source * bands + a, value, 0.0)
+                    n += 1
+        sums_ref[me, b] = jnp.concatenate(rows, axis=0) * (1.0 / (breadth * height * total))
+
+    def result_of(b):
+        def result(row, i, sums):
+            waves = Waves(me, row, i)
+            pairs = []
+            for p in range(2):
+                theta = theta_at(waves, p, row, i)
+                for c in range(3):
+                    theta_ref[p, c, b, row, rows_of(i), :] = theta[c]
+                pairs.append(waves.reduce(theta))
+            return add_sums(waves, pairs, row, i, sums)
+
+        return result
 
     def away_result(row, i, sums):
         waves = Waves(me, row, i)
@@ -781,41 +915,58 @@
         each_step(row, guest_result)
         return_copy(row).start()
 
-    each_row(guest_back)
-
-    def home_back(row, sums):
-        take_planes(0, row)
-        return each_sum(row, home_result, sums)
-
+    guest_back(0)
+    pl.when(outer)(start_home)
+    pl.when(inner)(lambda: guest_back(1))
     other_copy(side, 1).wait_recv()
     other_copy(1 - side, 0).wait_recv()
-    keep_sums(side, lax.fori_loop(0, depth, home_back, zero_sums()))
-
-    for part in range(2):
-        half_copy(mine, part).wait_send()
+
+    def take_direct():
+        each_of(members, lambda n: result_arrival(n).wait_recv())
+        planes_back(lambda c, p: in3_ref[:, c, p], 1)
+        each_sum(1, 1 - side, result_of(1 - side))
+
+    pl.when(inner)(take_direct)
+
+    def home_back(row):
+        take_planes(0, row)
+        each_sum(row, side, result_of(side))
+
+    home_back(0)
+    home_back(1)
+    keep_sums(side)
+
+    def away_back(row):
+        return_copy(row).wait_recv()
+        each_sum(row, 1 - side, away_result)
+
+    away_back(0)
+    pl.when(outer)(lambda: away_back(1))
+    keep_sums(1 - side)
+    each_peer(lambda k, peer, source: sums_copy(me, peer, k).start())
+    half_copy(mine, side).wait_send()
+    half_copy(mine, 1 - side).wait_send()
     each_peer(lambda k, peer, source: slab_copy(peer, me, k).wait_send())
-    for row in range(depth):
-        swap_copy(row).wait_send()
     other_copy(1 - side, 0).wait_send()
     other_copy(side, 1).wait_send()
-
-    def drain(row):
-        for s in range(2):
-            drain_all(*first, s, row, ends1(s))
-            drain_all(*second, s, row, ends2(s))
-
-    each_row(drain)
-
-    def away_back(row, sums):
-        return_copy(row).wait_recv()
-        return each_sum(row, away_result, sums)
-
-    keep_sums(1 - side, lax.fori_loop(0, depth, away_back, zero_sums()))
-    each_peer(lambda k, peer, source: sums_copy(me, peer, k).start())
-    for row in range(depth):
-        return_copy(row).wait_send()
+    swap_copy(0).wait_send()
+    return_copy(0).wait_send()
+    pl.when(jnp.logical_not(direct))(lambda: swap_copy(1).wait_send())
+
+    pl.when(direct)(lambda: each_of(members, lambda n: direct_copy(n).wait_send()))
+    pl.when(second_guest)(lambda: drain_all(*first, 1, 1, ends1(1)))
+    pl.when(inner)(lambda: return_copy(1).wait_send())
+    each_inner(lambda k, peer: to_peer(*second, 1, 1, k, peer, *ends2(1)).wait_send())
+    each_of(pack, lambda n: direct_result(n).wait_send())
+    drain_all(*first, 1, 0, ends1(1))
+    drain_all(*second, 1, 0, ends2(1))
+    each_row(lambda row: drain_all(*first, 0, row, ends1(0)))
+    each_row(lambda row: drain_all(*second, 0, row, ends2(0)))
     each_peer(lambda k, peer, source: sums_copy(source, source, k).wait_recv())
-    gram_ref[...] = jnp.sum(sums_ref[...], axis=0)
+    grams = jnp.sum(sums_ref[...], axis=0)
+    for p in range(2):
+        for b in range(bands):
+            gram_ref[p, b : b + 1, :] = grams[b, p : p + 1, : 2 * bands]
     each_peer(lambda k, peer, source: sums_copy(me, peer, k).wait_send())
 
 
@@ -826,7 +977,6 @@
     members = groups // 2
     columns = height // members
     table = jnp.asarray(split_table(breadth, total**-0.25))
-    grams = bands * 4 * bands
     voxels = (3, 2, total, columns, breadth)
     block = (2, depth, members, 3, 2, columns, breadth)
     pairs = (depth, 2, 2, height, breadth)
@@ -837,11 +987,11 @@
         pltpu.with_memory_space_constraint(v, pltpu.HBM)
         for v in (coeffs, material, inv_diag, inv_off, table)
     ]
-    theta, sums = pl.pallas_call(
+    theta, gram = pl.pallas_call(
         functools.partial(operator_kernel, groups),
         out_shape=(
             jax.ShapeDtypeStruct(coeffs.shape, single),
-            jax.ShapeDtypeStruct((grams, breadth), single),
+            jax.ShapeDtypeStruct((2, bands, 2 * bands), single),
         ),
         in_specs=[hbm, hbm, hbm, hbm, hbm],
         out_specs=(vmem, vmem),
@@ -867,8 +1017,11 @@
             pltpu.VMEM(voxels, single),
             pltpu.VMEM(block, single),
             pltpu.VMEM(block, single),
-            pltpu.VMEM((groups, grams, breadth), single),
-            dma((6,)),
+            pltpu.VMEM(block[2:], single),
+            pltpu.VMEM(block[2:], single),
+            pltpu.VMEM((bands, 4 * bands, 16, breadth), single),
+            pltpu.VMEM((groups, bands, 2, breadth), single),
+            dma((4, depth)),
             dma((groups,)),
             dma((groups,)),
             dma((2, 2)),
@@ -876,6 +1029,10 @@
             dma((2, depth, members)),
             dma((2, depth, members)),
             dma((2, depth, members)),
+            dma((members,)),
+            dma((members // 4,)),
+            dma((members // 2,)),
+            dma((members,)),
             dma((depth,)),
             dma((depth,)),
             dma((depth,)),
@@ -890,12 +1047,7 @@
         ),
         name="maxwell",
     )(*operands)
-    values = jnp.sum(sums, axis=1) / (breadth * height * total)
-    values = values.reshape(bands, 2, bands, 2).transpose(1, 3, 2, 0)
-    own, other = values[0], values[1]
-    first = lax.axis_index("ba") == 0
-    gram = jnp.concatenate([jnp.where(first, own, other), jnp.where(first, other, own)], axis=1)
-    return (theta, gram)
+    return (theta, gram.transpose(0, 2, 1))
 
 
 def fits(coeffs):
@@ -905,7 +1057,7 @@
         lax.axis_size("ba") == 2
         and bands == 2
         and depth == 2
-        and groups >= 4
+        and groups >= 8
         and height % (4 * groups) == 0
         and height % 16 == 0
         and height == breadth

time: 81.9 us -> 78.1 us (0.954)
  Pallas kernels: 78.8 us -> 75.6 us
    pallas_call x1, Pallas kernels: 78.8 us -> 75.6 us  [on_device_kernel(): pl.pallas_call(functools.partial(operator_kernel, groups), out_shape=(jax...]
where the time goes in v5:
time: 78.1 us; the launch traced here: 78 us
  Pallas kernels  75.6 us (97%)
  local copies, waits for them, and re-layouts  1.72 us (2%)
    pallas_call x1, Pallas kernels, on_device_kernel(): pl.pallas_call(functools.partial(operator_kernel, groups), out_shape=(jax...  75.6 us
    unnamed x2, local copies, waits for them, and re-layouts  1.72 us

profile of v5, /device:TPU:0, one launch (start us, length us, event | category | flops | bytes accessed | tf_op | source)
XLA Modules:
  0.0 78.0 jit_solution(9142140772679260011)
XLA Ops:
  0.6 75.6 %maxwell.1 = (f32[2,3,2,2,128,128]{5,4,3,2,1,0:T(8,128)S(1)}, f32[2,2,4]{2,1,0:T(2,128)S(1)}) custom-call(f32[2,3,2,2,128,128]{5,4,3,2,1,0:T(8,128)} %coeffs_hbm.1, s32[2,128,128]{2,1,0:T(8,128)} %material_hbm.1, f32[4,3]{1,0:T(4,128)} %diag_hbm.1, f32[4,3]{1,0:T(4,128)} %off_hbm.1, bf16[4,256,256]{2,1,0:T(8,128)(2,1)} %constant.2.clone.table_hbm), custom_call_target="tpu_custom_call" | custom-call | tf_op jit(solution)/shard_map/maxwell/pallas_call | solution.py:990
  76.2 1.1 %copy.9 = f32[2,3,2,2,128,128]{5,4,3,2,1,0:T(8,128)} copy(f32[2,3,2,2,128,128]{5,4,3,2,1,0:T(8,128)S(1)} %get-tuple-element.8) | data formatting | bytes 3145728
  77.4 0.6 copy.10

commit v6 on v5

--- a/solution.py
+++ b/solution.py
@@ -253,6 +253,8 @@
     recv3,
     send4,
     recv4,
+    part_send,
+    part_recv,
     swap_send,
     swap_recv,
     return_send,
@@ -758,8 +760,7 @@
     each_second_source(lambda k, source: from_peer(*first, 1, 1, k, source, *ends1(1)).wait_recv())
     each_of(pack // 2, lambda n: direct_arrival(n).wait_recv())
 
-    def inverse(n, carry):
-        c, at = n // (columns // 8), part_of(n % (columns // 8))
+    def inverse(at, c):
         points = []
         for r in range(total):
             owner, row = r // depth, r % depth
@@ -768,33 +769,51 @@
         for z, (real, imag) in enumerate(to_voxels(points)):
             field_ref[c, 0, z, at] = real
             field_ref[c, 1, z, at] = imag
-        return carry
-
-    lax.fori_loop(0, 3 * (columns // 8), inverse, 0)
-
-    def scale(z, carry):
-        xx, yy, zz, xy, yz, zx = [tensor_ref[entry, z // depth, z % depth] for entry in range(6)]
+
+    def scale(at, z):
+        entries = [tensor_ref[entry, z // depth, z % depth, at] for entry in range(6)]
+        xx, yy, zz, xy, yz, zx = entries
         for p in range(2):
-            fx, fy, fz = [field_ref[c, p, z] for c in range(3)]
-            scaled_ref[0, p, z] = xx * fx + xy * fy + zx * fz
-            scaled_ref[1, p, z] = xy * fx + yy * fy + yz * fz
-            scaled_ref[2, p, z] = zx * fx + yz * fy + zz * fz
-        return carry
-
-    lax.fori_loop(0, total, scale, 0, unroll=2)
-
-    def forward(n, carry):
-        c, at = n // (columns // 8), part_of(n % (columns // 8))
+            fx, fy, fz = [field_ref[c, p, z, at] for c in range(3)]
+            scaled_ref[0, p, z, at] = xx * fx + xy * fy + zx * fz
+            scaled_ref[1, p, z, at] = xy * fx + yy * fy + yz * fz
+            scaled_ref[2, p, z, at] = zx * fx + yz * fy + zz * fz
+
+    def forward(at, c):
         points = [(scaled_ref[c, 0, z, at], scaled_ref[c, 1, z, at]) for z in range(total)]
         for r, (real, imag) in enumerate(to_waves(points)):
             owner, row = r // depth, r % depth
             where = (owner // members, row, owner % members, c)
             out2_ref[(*where, 0, at)] = real
             out2_ref[(*where, 1, at)] = imag
-        return carry
-
-    lax.fori_loop(0, 3 * (columns // 8), forward, 0)
-    start_all(*second, 1, 0, ends2(1))
+
+    parts = columns // 8
+
+    def part_copy(n, k, peer, other):
+        at = part_of(n)
+        return pltpu.make_async_remote_copy(
+            src_ref=out2_ref.at[1 - side, 0, peer, :, :, at],
+            dst_ref=in2_ref.at[1, 0, other, :, :, at],
+            send_sem=part_send.at[n, k],
+            recv_sem=part_recv.at[n, k],
+            device_id={"gz": side * members + peer},
+            device_id_type=MESH,
+        )
+
+    def voxel_part(n):
+        at = part_of(n)
+        each_of(3, functools.partial(inverse, at))
+
+        def scale_step(z, carry):
+            scale(at, z)
+            return carry
+
+        lax.fori_loop(0, total, scale_step, 0, unroll=4)
+        each_of(3, functools.partial(forward, at))
+        each_member(lambda k, peer, source: part_copy(n, k, peer, seat).start())
+
+    each_of(parts, voxel_part)
+    in2_ref[1, 0, seat] = out2_ref[1 - side, 0, seat]
     each_of(pack, lambda n: direct_result((seat + n) % pack).start())
     each_inner(lambda k, peer: to_peer(*second, 1, 1, k, peer, *ends2(1)).start())
 
@@ -803,10 +822,11 @@
 
     pl.when(inner)(keep_guest)
 
-    def start_home():
-        each_row(lambda row: start_all(*second, 0, row, ends2(0)))
-
-    pl.when(inner)(start_home)
+    def start_home(row):
+        start_all(*second, 0, row, ends2(0))
+
+    start_home(0)
+    pl.when(inner)(lambda: start_home(1))
     other_copy(1 - side, 0).start()
 
     def planes_back(get, row):
@@ -823,7 +843,6 @@
         back_ref[row] = product(plain_table(), halves(spread_blocks(wide)))
 
     def take_planes(s, row):
-        finish_all(*second, s, row, ends2(s))
         planes_back(lambda c, p: in2_ref[s, row, :, c, p], row)
 
     def theta_at(waves, p, row, i):
@@ -915,9 +934,17 @@
         each_step(row, guest_result)
         return_copy(row).start()
 
+    def finish_parts(n):
+        each_member(lambda k, peer, source: part_copy(n, k, source, source).wait_recv())
+
+    def second_back():
+        finish_all(*second, 1, 1, ends2(1))
+        guest_back(1)
+
+    each_of(parts, finish_parts)
     guest_back(0)
-    pl.when(outer)(start_home)
-    pl.when(inner)(lambda: guest_back(1))
+    pl.when(outer)(lambda: start_home(1))
+    pl.when(inner)(second_back)
     other_copy(side, 1).wait_recv()
     other_copy(1 - side, 0).wait_recv()
 
@@ -929,6 +956,7 @@
     pl.when(inner)(take_direct)
 
     def home_back(row):
+        finish_all(*second, 0, row, ends2(0))
         take_planes(0, row)
         each_sum(row, side, result_of(side))
 
@@ -959,7 +987,11 @@
     each_inner(lambda k, peer: to_peer(*second, 1, 1, k, peer, *ends2(1)).wait_send())
     each_of(pack, lambda n: direct_result(n).wait_send())
     drain_all(*first, 1, 0, ends1(1))
-    drain_all(*second, 1, 0, ends2(1))
+
+    def drain_parts(n):
+        each_member(lambda k, peer, source: part_copy(n, k, peer, seat).wait_send())
+
+    each_of(parts, drain_parts)
     each_row(lambda row: drain_all(*first, 0, row, ends1(0)))
     each_row(lambda row: drain_all(*second, 0, row, ends2(0)))
     each_peer(lambda k, peer, source: sums_copy(source, source, k).wait_recv())
@@ -968,6 +1000,19 @@
         for b in range(bands):
             gram_ref[p, b : b + 1, :] = grams[b, p : p + 1, : 2 * bands]
     each_peer(lambda k, peer, source: sums_copy(me, peer, k).wait_send())
+
+
+def deliver_kernel(theta_ref, gram_ref, theta_out, gram_out, theta_sem, gram_sem):
+    copies = [pltpu.make_async_copy(gram_ref, gram_out, gram_sem)]
+    for p in range(2):
+        for c in range(3):
+            copies.append(
+                pltpu.make_async_copy(theta_ref.at[p, c], theta_out.at[p, c], theta_sem.at[p, c])
+            )
+    for copy in copies:
+        copy.start()
+    for copy in copies:
+        copy.wait()
 
 
 def on_device_kernel(coeffs, material, inv_diag, inv_off):
@@ -1033,6 +1078,8 @@
             dma((members // 4,)),
             dma((members // 2,)),
             dma((members,)),
+            dma((columns // 8, members)),
+            dma((columns // 8, members)),
             dma((depth,)),
             dma((depth,)),
             dma((depth,)),
@@ -1047,6 +1094,18 @@
         ),
         name="maxwell",
     )(*operands)
+    theta, gram = pl.pallas_call(
+        deliver_kernel,
+        out_shape=(
+            jax.ShapeDtypeStruct(theta.shape, single),
+            jax.ShapeDtypeStruct(gram.shape, single),
+        ),
+        in_specs=[vmem, vmem],
+        out_specs=(hbm, hbm),
+        scratch_shapes=[dma((2, 3)), dma(())],
+        compiler_params=pltpu.CompilerParams(vmem_limit_bytes=8 * 1024 * 1024),
+        name="deliver",
+    )(theta, gram)
     return (theta, gram.transpose(0, 2, 1))
 
 

time: 78.1 us -> 76.8 us (0.983)
  local copies, waits for them, and re-layouts: 1.72 us -> 0 us
    unnamed x2 -> x0, local copies, waits for them, and re-layouts: 1.72 us -> none
    pallas_call x0 -> x1, Pallas kernels: none -> 1.2 us  [on_device_kernel(): pl.pallas_call(deliver_kernel, out_shape=(jax.ShapeDtypeStruct(theta.shap...]
    pallas_call x1, Pallas kernels: 75.6 us -> 74.8 us  [on_device_kernel(): pl.pallas_call(functools.partial(operator_kernel, groups), out_shape=(jax...]
where the time goes in v6:
time: 76.8 us; the launch traced here: 76.6 us
  Pallas kernels  76 us (99%)
    pallas_call x1, Pallas kernels, on_device_kernel(): pl.pallas_call(functools.partial(operator_kernel, groups), out_shape=(jax...  74.8 us

profile of v6, /device:TPU:0, one launch (start us, length us, event | category | flops | bytes accessed | tf_op | source)
XLA Modules:
  0.0 76.6 jit_solution(10880635985477219783)
XLA Ops:
  0.6 74.8 %maxwell.1 = (f32[2,3,2,2,128,128]{5,4,3,2,1,0:T(8,128)S(1)}, f32[2,2,4]{2,1,0:T(2,128)S(1)}) custom-call(f32[2,3,2,2,128,128]{5,4,3,2,1,0:T(8,128)} %coeffs_hbm.1, s32[2,128,128]{2,1,0:T(8,128)} %material_hbm.1, f32[4,3]{1,0:T(4,128)} %diag_hbm.1, f32[4,3]{1,0:T(4,128)} %off_hbm.1, bf16[4,256,256]{2,1,0:T(8,128)(2,1)} %constant.2.clone.table_hbm), custom_call_target="tpu_custom_call" | custom-call | tf_op jit(solution)/shard_map/maxwell/pallas_call | solution.py:1035
  75.4 1.2 %deliver.1 = (f32[2,3,2,2,128,128]{5,4,3,2,1,0:T(8,128)}, f32[2,2,4]{2,1,0:T(2,128)}) custom-call(f32[2,3,2,2,128,128]{5,4,3,2,1,0:T(8,128)S(1)} %get-tuple-element.6.theta_ref, f32[2,2,4]{2,1,0:T(2,128)S(1)} %get-tuple-element.7.gram_ref), custom_call_target="tpu_custom_call" | custom-call | tf_op jit(solution)/shard_map/deliver/pallas_call | solution.py:1097

commit v7 on v6

--- a/solution.py
+++ b/solution.py
@@ -249,20 +249,14 @@
     recv1,
     send2,
     recv2,
-    send3,
-    recv3,
-    send4,
-    recv4,
-    part_send,
-    part_recv,
+    far_sem,
     swap_send,
     swap_recv,
     return_send,
     return_recv,
     other_send,
     other_recv,
-    sums_send,
-    sums_recv,
+    sums_sem,
 ):
     _, comps, bands, depth, height, breadth = coeffs_ref.shape
     total = depth * groups
@@ -286,21 +280,21 @@
 
     def each_peer(body):
         def step(k, carry):
-            body(k, (me + k) % groups, (me + groups - k) % groups)
+            body((me + k) % groups)
             return carry
 
         lax.fori_loop(1, groups, step, 0)
 
     def each_member(body):
         def step(k, carry):
-            body(k, (seat + k) % members, (seat + members - k) % members)
+            body(k, (seat + k) % members)
             return carry
 
         lax.fori_loop(1, members, step, 0)
 
     barrier = pltpu.get_barrier_semaphore()
     each_peer(
-        lambda k, peer, source: pl.semaphore_signal(
+        lambda peer: pl.semaphore_signal(
             barrier, inc=1, device_id={"gz": peer}, device_id_type=MESH
         )
     )
@@ -480,23 +474,23 @@
             axis=0,
         )
 
-    def to_peer(out, into, send, recv, s, row, k, peer, from_at, to_at):
+    def to_peer(out, into, send, recv, s, row, peer, from_at, to_at):
         return pltpu.make_async_remote_copy(
             src_ref=out.at[from_at, row, peer],
             dst_ref=into.at[to_at, row, seat],
-            send_sem=send.at[s, row, k],
-            recv_sem=recv.at[s, row, k],
+            send_sem=send.at[s, row],
+            recv_sem=recv.at[s, row],
             device_id={"gz": side * members + peer},
             device_id_type=MESH,
         )
 
-    def from_peer(out, into, send, recv, s, row, k, source, from_at, to_at):
-        return pltpu.make_async_remote_copy(
-            src_ref=out.at[from_at, row, source],
-            dst_ref=into.at[to_at, row, source],
-            send_sem=send.at[s, row, k],
-            recv_sem=recv.at[s, row, k],
-            device_id={"gz": side * members + source},
+    def blocks(count, out, into, send, recv, s, row, from_at, to_at):
+        return pltpu.make_async_remote_copy(
+            src_ref=out.at[from_at, row, pl.ds(0, count)],
+            dst_ref=into.at[to_at, row, pl.ds(0, count)],
+            send_sem=send.at[s, row],
+            recv_sem=recv.at[s, row],
+            device_id={"gz": side * members + (seat + 1) % members},
             device_id_type=MESH,
         )
 
@@ -507,26 +501,21 @@
         return (side + s) % 2, s
 
     def start_all(out, into, send, recv, s, row, ends):
-        each_member(
-            lambda k, peer, source: to_peer(
-                out, into, send, recv, s, row, k, peer, *ends
-            ).start()
-        )
+        each_member(lambda k, peer: to_peer(out, into, send, recv, s, row, peer, *ends).start())
         into[ends[1], row, seat] = out[ends[0], row, seat]
+
+    def finish_all(out, into, send, recv, s, row, ends):
+        blocks(members - 1, out, into, send, recv, s, row, *ends).wait_recv()
+
+    def drain_all(out, into, send, recv, s, row, ends):
+        blocks(members - 1, out, into, send, recv, s, row, *ends).wait_send()
 
     def is_inner(peer):
         return peer // pack == 1 - side
 
     def each_inner(body):
-        def one(k, peer, source):
+        def one(k, peer):
             pl.when(is_inner(peer))(lambda: body(k, peer))
-
-        each_member(one)
-
-    def each_second_source(body):
-        def one(k, peer, source):
-            has_guest = jnp.logical_or(is_inner(source), source % 2 == 1)
-            pl.when(has_guest)(lambda: body(k, source))
 
         each_member(one)
 
@@ -537,20 +526,19 @@
         return pltpu.make_async_remote_copy(
             src_ref=out3_ref.at[peer],
             dst_ref=in1_ref.at[side, 1, seat],
-            send_sem=send3.at[peer],
-            recv_sem=recv3.at[seat % pack // 2],
+            send_sem=far_sem.at[0],
+            recv_sem=far_sem.at[1],
             device_id=across(peer),
             device_id_type=MESH,
         )
 
-    def direct_arrival(n):
-        source = side * pack + 2 * n
-        return pltpu.make_async_remote_copy(
-            src_ref=out3_ref.at[source],
-            dst_ref=in1_ref.at[1 - side, 1, source],
-            send_sem=send3.at[source],
-            recv_sem=recv3.at[n],
-            device_id=across(source),
+    def direct_blocks(count):
+        return pltpu.make_async_remote_copy(
+            src_ref=out3_ref.at[pl.ds(0, count)],
+            dst_ref=in1_ref.at[1 - side, 1, pl.ds(0, count)],
+            send_sem=far_sem.at[0],
+            recv_sem=far_sem.at[1],
+            device_id=across(seat),
             device_id_type=MESH,
         )
 
@@ -559,19 +547,19 @@
         return pltpu.make_async_remote_copy(
             src_ref=out2_ref.at[1 - side, 1, peer],
             dst_ref=in3_ref.at[seat],
-            send_sem=send4.at[n],
-            recv_sem=recv4.at[seat],
+            send_sem=far_sem.at[2],
+            recv_sem=far_sem.at[3],
             device_id=across(peer),
             device_id_type=MESH,
         )
 
-    def result_arrival(source):
-        return pltpu.make_async_remote_copy(
-            src_ref=out2_ref.at[1 - side, 1, source],
-            dst_ref=in3_ref.at[source],
-            send_sem=send4.at[source % pack],
-            recv_sem=recv4.at[source],
-            device_id=across(source),
+    def result_blocks(count):
+        return pltpu.make_async_remote_copy(
+            src_ref=out2_ref.at[1 - side, 1, pl.ds(0, count)],
+            dst_ref=in3_ref.at[pl.ds(0, count)],
+            send_sem=far_sem.at[2],
+            recv_sem=far_sem.at[3],
+            device_id=across(seat),
             device_id_type=MESH,
         )
 
@@ -581,20 +569,6 @@
             return carry
 
         lax.fori_loop(0, count, step, 0)
-
-    def finish_all(out, into, send, recv, s, row, ends):
-        each_member(
-            lambda k, peer, source: from_peer(
-                out, into, send, recv, s, row, k, source, *ends
-            ).wait_recv()
-        )
-
-    def drain_all(out, into, send, recv, s, row, ends):
-        each_member(
-            lambda k, peer, source: to_peer(
-                out, into, send, recv, s, row, k, peer, *ends
-            ).wait_send()
-        )
 
     first = (out1_ref, in1_ref, send1, recv1)
     second = (out2_ref, in2_ref, send2, recv2)
@@ -646,13 +620,24 @@
     def columns_of(peer):
         return pl.ds(pl.multiple_of((peer % members) * columns, columns), columns)
 
-    def slab_copy(peer, slot, k):
+    def slab_copy(peer, n):
         return pltpu.make_async_remote_copy(
             src_ref=material_ref.at[mine, columns_of(peer), :],
-            dst_ref=slab_ref.at[mine, slot],
-            send_sem=slab_send.at[k],
-            recv_sem=slab_recv.at[k],
+            dst_ref=slab_ref.at[mine, me],
+            send_sem=slab_send.at[n],
+            recv_sem=slab_recv.at[n],
             device_id={"gz": peer},
+            device_id_type=MESH,
+        )
+
+    def slab_blocks(n):
+        slots = slab_ref.at[mine, pl.ds(0, members - 1 + n)]
+        return pltpu.make_async_remote_copy(
+            src_ref=slots,
+            dst_ref=slots,
+            send_sem=slab_send.at[n],
+            recv_sem=slab_recv.at[n],
+            device_id={"gz": partner},
             device_id_type=MESH,
         )
 
@@ -677,29 +662,20 @@
         make_planes(0, row)
         start_all(*first, 0, row, ends1(0))
 
-    def start_slabs(base):
+    def start_slab(base, n):
         def step(k, carry):
-            peer = base * members + (seat + k) % members
-            slab_copy(peer, me, (peer + groups - me) % groups).start()
+            slab_copy(base * members + (seat + k) % members, n).start()
             return carry
 
-        return step
-
-    def wait_slabs(base):
-        def step(k, carry):
-            source = base * members + (seat + members - k) % members
-            slab_copy(source, source, (me + groups - source) % groups).wait_recv()
-            return carry
-
-        return step
+        lax.fori_loop(1 - n, members, step, 0)
 
     away_row(0)
     pl.semaphore_wait(barrier, groups)
     swap_copy(0).start()
     for load in loads:
         load.wait()
-    lax.fori_loop(1, members, start_slabs(side), 0)
-    lax.fori_loop(0, members, start_slabs(1 - side), 0)
+    start_slab(side, 0)
+    start_slab(1 - side, 1)
     away_row(1)
     pl.when(jnp.logical_not(direct))(lambda: swap_copy(1).start())
     slab_ref[mine, me] = material_ref[mine, columns_of(me), :]
@@ -728,10 +704,10 @@
         start_all(*first, 1, row, ends1(1))
 
     guest_row(0)
-    lax.fori_loop(1, members, wait_slabs(side), 0)
+    slab_blocks(0).wait_recv()
     half_copy(mine, side).start()
     pl.when(inner)(lambda: guest_row(1))
-    lax.fori_loop(0, members, wait_slabs(1 - side), 0)
+    slab_blocks(1).wait_recv()
     half_copy(mine, 1 - side).start()
     pl.when(direct)(send_direct)
     pl.when(jnp.logical_and(outer, odd))(lambda: guest_row(1))
@@ -757,8 +733,14 @@
 
     each_row(lambda row: finish_all(*first, 0, row, ends1(0)))
     finish_all(*first, 1, 0, ends1(1))
-    each_second_source(lambda k, source: from_peer(*first, 1, 1, k, source, *ends1(1)).wait_recv())
-    each_of(pack // 2, lambda n: direct_arrival(n).wait_recv())
+
+    def finish_second(count):
+        blocks(count, *first, 1, 1, *ends1(1)).wait_recv()
+
+    guests = pack + pack // 2
+    pl.when(second_guest)(lambda: finish_second(guests - 1))
+    pl.when(jnp.logical_not(second_guest))(lambda: finish_second(guests))
+    direct_blocks(pack // 2).wait_recv()
 
     def inverse(at, c):
         points = []
@@ -789,13 +771,13 @@
 
     parts = columns // 8
 
-    def part_copy(n, k, peer, other):
+    def part_copy(n, peer):
         at = part_of(n)
         return pltpu.make_async_remote_copy(
             src_ref=out2_ref.at[1 - side, 0, peer, :, :, at],
-            dst_ref=in2_ref.at[1, 0, other, :, :, at],
-            send_sem=part_send.at[n, k],
-            recv_sem=part_recv.at[n, k],
+            dst_ref=in2_ref.at[1, 0, seat, :, :, at],
+            send_sem=send2.at[1, 0],
+            recv_sem=recv2.at[1, 0],
             device_id={"gz": side * members + peer},
             device_id_type=MESH,
         )
@@ -810,12 +792,12 @@
 
         lax.fori_loop(0, total, scale_step, 0, unroll=4)
         each_of(3, functools.partial(forward, at))
-        each_member(lambda k, peer, source: part_copy(n, k, peer, seat).start())
+        each_member(lambda k, peer: part_copy(n, peer).start())
 
     each_of(parts, voxel_part)
     in2_ref[1, 0, seat] = out2_ref[1 - side, 0, seat]
     each_of(pack, lambda n: direct_result((seat + n) % pack).start())
-    each_inner(lambda k, peer: to_peer(*second, 1, 1, k, peer, *ends2(1)).start())
+    each_inner(lambda k, peer: to_peer(*second, 1, 1, peer, *ends2(1)).start())
 
     def keep_guest():
         in2_ref[1, 1, seat] = out2_ref[1 - side, 1, seat]
@@ -919,13 +901,24 @@
             pairs.append(pair)
         return add_sums(waves, pairs, row, i, sums)
 
-    def sums_copy(slot, peer, k):
-        return pltpu.make_async_remote_copy(
-            src_ref=sums_ref.at[slot],
-            dst_ref=sums_ref.at[slot],
-            send_sem=sums_send.at[k],
-            recv_sem=sums_recv.at[k],
+    def sums_copy(peer):
+        return pltpu.make_async_remote_copy(
+            src_ref=sums_ref.at[me],
+            dst_ref=sums_ref.at[me],
+            send_sem=sums_sem.at[0],
+            recv_sem=sums_sem.at[1],
             device_id={"gz": peer},
+            device_id_type=MESH,
+        )
+
+    def sums_blocks():
+        slots = sums_ref.at[pl.ds(0, groups - 1)]
+        return pltpu.make_async_remote_copy(
+            src_ref=slots,
+            dst_ref=slots,
+            send_sem=sums_sem.at[0],
+            recv_sem=sums_sem.at[1],
+            device_id={"gz": partner},
             device_id_type=MESH,
         )
 
@@ -934,14 +927,11 @@
         each_step(row, guest_result)
         return_copy(row).start()
 
-    def finish_parts(n):
-        each_member(lambda k, peer, source: part_copy(n, k, source, source).wait_recv())
-
     def second_back():
         finish_all(*second, 1, 1, ends2(1))
         guest_back(1)
 
-    each_of(parts, finish_parts)
+    finish_all(*second, 1, 0, ends2(1))
     guest_back(0)
     pl.when(outer)(lambda: start_home(1))
     pl.when(inner)(second_back)
@@ -949,7 +939,7 @@
     other_copy(1 - side, 0).wait_recv()
 
     def take_direct():
-        each_of(members, lambda n: result_arrival(n).wait_recv())
+        result_blocks(members).wait_recv()
         planes_back(lambda c, p: in3_ref[:, c, p], 1)
         each_sum(1, 1 - side, result_of(1 - side))
 
@@ -971,35 +961,33 @@
     away_back(0)
     pl.when(outer)(lambda: away_back(1))
     keep_sums(1 - side)
-    each_peer(lambda k, peer, source: sums_copy(me, peer, k).start())
+    each_peer(lambda peer: sums_copy(peer).start())
     half_copy(mine, side).wait_send()
     half_copy(mine, 1 - side).wait_send()
-    each_peer(lambda k, peer, source: slab_copy(peer, me, k).wait_send())
+    slab_blocks(0).wait_send()
+    slab_blocks(1).wait_send()
     other_copy(1 - side, 0).wait_send()
     other_copy(side, 1).wait_send()
     swap_copy(0).wait_send()
     return_copy(0).wait_send()
     pl.when(jnp.logical_not(direct))(lambda: swap_copy(1).wait_send())
 
-    pl.when(direct)(lambda: each_of(members, lambda n: direct_copy(n).wait_send()))
+    pl.when(direct)(lambda: direct_blocks(members).wait_send())
     pl.when(second_guest)(lambda: drain_all(*first, 1, 1, ends1(1)))
     pl.when(inner)(lambda: return_copy(1).wait_send())
-    each_inner(lambda k, peer: to_peer(*second, 1, 1, k, peer, *ends2(1)).wait_send())
-    each_of(pack, lambda n: direct_result(n).wait_send())
+    pl.when(inner)(lambda: blocks(pack - 1, *second, 1, 1, *ends2(1)).wait_send())
+    pl.when(outer)(lambda: blocks(pack, *second, 1, 1, *ends2(1)).wait_send())
+    result_blocks(pack).wait_send()
     drain_all(*first, 1, 0, ends1(1))
-
-    def drain_parts(n):
-        each_member(lambda k, peer, source: part_copy(n, k, peer, seat).wait_send())
-
-    each_of(parts, drain_parts)
+    drain_all(*second, 1, 0, ends2(1))
     each_row(lambda row: drain_all(*first, 0, row, ends1(0)))
     each_row(lambda row: drain_all(*second, 0, row, ends2(0)))
-    each_peer(lambda k, peer, source: sums_copy(source, source, k).wait_recv())
+    sums_blocks().wait_recv()
     grams = jnp.sum(sums_ref[...], axis=0)
     for p in range(2):
         for b in range(bands):
             gram_ref[p, b : b + 1, :] = grams[b, p : p + 1, : 2 * bands]
-    each_peer(lambda k, peer, source: sums_copy(me, peer, k).wait_send())
+    sums_blocks().wait_send()
 
 
 def deliver_kernel(theta_ref, gram_ref, theta_out, gram_out, theta_sem, gram_sem):
@@ -1067,27 +1055,21 @@
             pltpu.VMEM((bands, 4 * bands, 16, breadth), single),
             pltpu.VMEM((groups, bands, 2, breadth), single),
             dma((4, depth)),
-            dma((groups,)),
-            dma((groups,)),
+            dma((2,)),
+            dma((2,)),
             dma((2, 2)),
-            dma((2, depth, members)),
-            dma((2, depth, members)),
-            dma((2, depth, members)),
-            dma((2, depth, members)),
-            dma((members,)),
-            dma((members // 4,)),
-            dma((members // 2,)),
-            dma((members,)),
-            dma((columns // 8, members)),
-            dma((columns // 8, members)),
+            dma((2, depth)),
+            dma((2, depth)),
+            dma((2, depth)),
+            dma((2, depth)),
+            dma((4,)),
             dma((depth,)),
             dma((depth,)),
             dma((depth,)),
             dma((depth,)),
             dma((2,)),
             dma((2,)),
-            dma((groups,)),
-            dma((groups,)),
+            dma((2,)),
         ],
         compiler_params=pltpu.CompilerParams(
             collective_id=0, has_side_effects=True, vmem_limit_bytes=48 * 1024 * 1024

time: 76.8 us -> 74.6 us (0.971)
  Pallas kernels: 76 us -> 73.8 us
    pallas_call x1, Pallas kernels: 74.8 us -> 72.6 us  [on_device_kernel(): pl.pallas_call(functools.partial(operator_kernel, groups), out_shape=(jax...]
where the time goes in v7:
time: 74.6 us; the launch traced here: 74.4 us
  Pallas kernels  73.8 us (99%)
    pallas_call x1, Pallas kernels, on_device_kernel(): pl.pallas_call(functools.partial(operator_kernel, groups), out_shape=(jax...  72.6 us

profile of v7, /device:TPU:0, one launch (start us, length us, event | category | flops | bytes accessed | tf_op | source)
XLA Modules:
  0.0 74.4 jit_solution(12326764284772501187)
XLA Ops:
  0.6 72.6 %maxwell.1 = (f32[2,3,2,2,128,128]{5,4,3,2,1,0:T(8,128)S(1)}, f32[2,2,4]{2,1,0:T(2,128)S(1)}) custom-call(f32[2,3,2,2,128,128]{5,4,3,2,1,0:T(8,128)} %coeffs_hbm.1, s32[2,128,128]{2,1,0:T(8,128)} %material_hbm.1, f32[4,3]{1,0:T(4,128)} %diag_hbm.1, f32[4,3]{1,0:T(4,128)} %off_hbm.1, bf16[4,256,256]{2,1,0:T(8,128)(2,1)} %constant.2.clone.table_hbm), custom_call_target="tpu_custom_call" | custom-call | tf_op jit(solution)/shard_map/maxwell/pallas_call | solution.py:1023
  73.2 1.2 %deliver.1 = (f32[2,3,2,2,128,128]{5,4,3,2,1,0:T(8,128)}, f32[2,2,4]{2,1,0:T(2,128)}) custom-call(f32[2,3,2,2,128,128]{5,4,3,2,1,0:T(8,128)S(1)} %get-tuple-element.6.theta_ref, f32[2,2,4]{2,1,0:T(2,128)S(1)} %get-tuple-element.7.gram_ref), custom_call_target="tpu_custom_call" | custom-call | tf_op jit(solution)/shard_map/deliver/pallas_call | solution.py:1079

commit v8 on v7

--- a/solution.py
+++ b/solution.py
@@ -292,14 +292,6 @@
 
         lax.fori_loop(1, members, step, 0)
 
-    barrier = pltpu.get_barrier_semaphore()
-    each_peer(
-        lambda peer: pl.semaphore_signal(
-            barrier, inc=1, device_id={"gz": peer}, device_id_type=MESH
-        )
-    )
-    pl.semaphore_signal(barrier, inc=1, device_id=mate, device_id_type=MESH)
-
     def row_load(b, row, n):
         return pltpu.make_async_copy(
             coeffs_hbm.at[:, :, b, row], coeffs_ref.at[:, :, b, row], load_sem.at[n, row]
@@ -311,8 +303,16 @@
         pltpu.make_async_copy(diag_hbm, diag_ref, load_sem.at[3, 0]),
         pltpu.make_async_copy(off_hbm, off_ref, load_sem.at[3, 1]),
     ]
-    for row in range(depth):
-        row_load(1 - side, row, 0).start()
+    row_load(1 - side, 0, 0).start()
+    barrier = pltpu.get_barrier_semaphore()
+    each_peer(
+        lambda peer: pl.semaphore_signal(
+            barrier, inc=1, device_id={"gz": peer}, device_id_type=MESH
+        )
+    )
+    pl.semaphore_signal(barrier, inc=1, device_id=mate, device_id_type=MESH)
+
+    row_load(1 - side, 1, 0).start()
     for row in range(depth):
         row_load(side, row, 1).start()
     for load in loads:
@@ -674,10 +674,12 @@
     swap_copy(0).start()
     for load in loads:
         load.wait()
-    start_slab(side, 0)
-    start_slab(1 - side, 1)
+    pl.when(inner)(lambda: start_slab(side, 0))
+    pl.when(inner)(lambda: start_slab(1 - side, 1))
     away_row(1)
     pl.when(jnp.logical_not(direct))(lambda: swap_copy(1).start())
+    pl.when(outer)(lambda: start_slab(side, 0))
+    pl.when(outer)(lambda: start_slab(1 - side, 1))
     slab_ref[mine, me] = material_ref[mine, columns_of(me), :]
     home_row(0)
     home_row(1)
@@ -807,7 +809,7 @@
     def start_home(row):
         start_all(*second, 0, row, ends2(0))
 
-    start_home(0)
+    pl.when(inner)(lambda: start_home(0))
     pl.when(inner)(lambda: start_home(1))
     other_copy(1 - side, 0).start()
 
@@ -933,6 +935,7 @@
 
     finish_all(*second, 1, 0, ends2(1))
     guest_back(0)
+    pl.when(outer)(lambda: start_home(0))
     pl.when(outer)(lambda: start_home(1))
     pl.when(inner)(second_back)
     other_copy(side, 1).wait_recv()
@@ -950,18 +953,33 @@
         take_planes(0, row)
         each_sum(row, side, result_of(side))
 
-    home_back(0)
-    home_back(1)
-    keep_sums(side)
-
     def away_back(row):
         return_copy(row).wait_recv()
         each_sum(row, 1 - side, away_result)
 
-    away_back(0)
-    pl.when(outer)(lambda: away_back(1))
-    keep_sums(1 - side)
-    each_peer(lambda peer: sums_copy(peer).start())
+    def finish_inner():
+        away_back(0)
+        keep_sums(1 - side)
+        home_back(1)
+        keep_sums(side)
+
+    def finish_outer():
+        home_back(1)
+        keep_sums(side)
+        away_back(0)
+        away_back(1)
+        keep_sums(1 - side)
+
+    home_back(0)
+    pl.when(inner)(finish_inner)
+    pl.when(outer)(finish_outer)
+
+    def start_sums(n, carry):
+        peer = (2 * groups - 1 - me + n) % groups
+        pl.when(peer != me)(lambda: sums_copy(peer).start())
+        return carry
+
+    lax.fori_loop(0, groups, start_sums, 0)
     half_copy(mine, side).wait_send()
     half_copy(mine, 1 - side).wait_send()
     slab_blocks(0).wait_send()

time: 74.6 us -> 74.1 us (level)
  no operation moved by 1% of the time
where the time goes in v8:
time: 74.1 us; the launch traced here: 74 us
  Pallas kernels  73.4 us (99%)
    pallas_call x1, Pallas kernels, on_device_kernel(): pl.pallas_call(functools.partial(operator_kernel, groups), out_shape=(jax...  72.2 us

profile of v8, /device:TPU:0, one launch (start us, length us, event | category | flops | bytes accessed | tf_op | source)
XLA Modules:
  0.0 74.0 jit_solution(2617186716543895532)
XLA Ops:
  0.6 72.2 %maxwell.1 = (f32[2,3,2,2,128,128]{5,4,3,2,1,0:T(8,128)S(1)}, f32[2,2,4]{2,1,0:T(2,128)S(1)}) custom-call(f32[2,3,2,2,128,128]{5,4,3,2,1,0:T(8,128)} %coeffs_hbm.1, s32[2,128,128]{2,1,0:T(8,128)} %material_hbm.1, f32[4,3]{1,0:T(4,128)} %diag_hbm.1, f32[4,3]{1,0:T(4,128)} %off_hbm.1, bf16[4,256,256]{2,1,0:T(8,128)(2,1)} %constant.2.clone.table_hbm), custom_call_target="tpu_custom_call" | custom-call | tf_op jit(solution)/shard_map/maxwell/pallas_call | solution.py:1041
  72.8 1.2 %deliver.1 = (f32[2,3,2,2,128,128]{5,4,3,2,1,0:T(8,128)}, f32[2,2,4]{2,1,0:T(2,128)}) custom-call(f32[2,3,2,2,128,128]{5,4,3,2,1,0:T(8,128)S(1)} %get-tuple-element.6.theta_ref, f32[2,2,4]{2,1,0:T(2,128)S(1)} %get-tuple-element.7.gram_ref), custom_call_target="tpu_custom_call" | custom-call | tf_op jit(solution)/shard_map/deliver/pallas_call | solution.py:1097

commit v9 on v8

--- a/solution.py
+++ b/solution.py
@@ -389,7 +389,7 @@
             body(row, i)
             return carry
 
-        lax.fori_loop(0, steps, step, 0)
+        lax.fori_loop(0, steps, step, 0, unroll=2)
 
     def each_row(body):
         def step(row, carry):
@@ -861,7 +861,7 @@
         def step(i, sums):
             return body(row, i, sums)
 
-        sums = lax.fori_loop(0, steps, step, tuple(acc_ref[b, n] for n in range(4 * bands)))
+        sums = lax.fori_loop(0, steps, step, tuple(acc_ref[b, n] for n in range(4 * bands)), unroll=2)
         for n in range(4 * bands):
             acc_ref[b, n] = sums[n]
 
@@ -979,7 +979,7 @@
         pl.when(peer != me)(lambda: sums_copy(peer).start())
         return carry
 
-    lax.fori_loop(0, groups, start_sums, 0)
+    lax.fori_loop(0, groups, start_sums, 0, unroll=True)
     half_copy(mine, side).wait_send()
     half_copy(mine, 1 - side).wait_send()
     slab_blocks(0).wait_send()
@@ -1011,10 +1011,7 @@
 def deliver_kernel(theta_ref, gram_ref, theta_out, gram_out, theta_sem, gram_sem):
     copies = [pltpu.make_async_copy(gram_ref, gram_out, gram_sem)]
     for p in range(2):
-        for c in range(3):
-            copies.append(
-                pltpu.make_async_copy(theta_ref.at[p, c], theta_out.at[p, c], theta_sem.at[p, c])
-            )
+        copies.append(pltpu.make_async_copy(theta_ref.at[p], theta_out.at[p], theta_sem.at[p]))
     for copy in copies:
         copy.start()
     for copy in copies:
@@ -1102,7 +1099,7 @@
         ),
         in_specs=[vmem, vmem],
         out_specs=(hbm, hbm),
-        scratch_shapes=[dma((2, 3)), dma(())],
+        scratch_shapes=[dma((2,)), dma(())],
         compiler_params=pltpu.CompilerParams(vmem_limit_bytes=8 * 1024 * 1024),
         name="deliver",
     )(theta, gram)

time: 74.1 us -> 73.9 us (level)
  no operation moved by 1% of the time
where the time goes in v9:
time: 73.9 us; the launch traced here: 73.8 us
  Pallas kernels  73.1 us (99%)
    pallas_call x1, Pallas kernels, on_device_kernel(): pl.pallas_call(functools.partial(operator_kernel, groups), out_shape=(jax...  72 us

profile of v9, /device:TPU:0, one launch (start us, length us, event | category | flops | bytes accessed | tf_op | source)
XLA Modules:
  0.0 73.8 jit_solution(9925425616106923445)
XLA Ops:
  0.6 72.0 %maxwell.1 = (f32[2,3,2,2,128,128]{5,4,3,2,1,0:T(8,128)S(1)}, f32[2,2,4]{2,1,0:T(2,128)S(1)}) custom-call(f32[2,3,2,2,128,128]{5,4,3,2,1,0:T(8,128)} %coeffs_hbm.1, s32[2,128,128]{2,1,0:T(8,128)} %material_hbm.1, f32[4,3]{1,0:T(4,128)} %diag_hbm.1, f32[4,3]{1,0:T(4,128)} %off_hbm.1, bf16[4,256,256]{2,1,0:T(8,128)(2,1)} %constant.2.clone.table_hbm), custom_call_target="tpu_custom_call" | custom-call | tf_op jit(solution)/shard_map/maxwell/pallas_call | solution.py:1038
  72.6 1.2 %deliver.1 = (f32[2,3,2,2,128,128]{5,4,3,2,1,0:T(8,128)}, f32[2,2,4]{2,1,0:T(2,128)}) custom-call(f32[2,3,2,2,128,128]{5,4,3,2,1,0:T(8,128)S(1)} %get-tuple-element.6.theta_ref, f32[2,2,4]{2,1,0:T(2,128)S(1)} %get-tuple-element.7.gram_ref), custom_call_target="tpu_custom_call" | custom-call | tf_op jit(solution)/shard_map/deliver/pallas_call | solution.py:1094
